TPU v7x, 32 devices: a whole 2x2x4 slice. The times are simulated.
32 devices in a mesh: frames: 2 (over x), date: 8 (over z, y), row: 2 (over core).
Axes of the slice: x: 2, y: 2, z: 4, core: 2. Of those that a mesh axis runs over, the one named last changes fastest.
Arguments:
- intensity: float32 [128, 512, 512], P(('frames', 'date'), 'row'), parts along dimension 0, may hold values from 0.05 to 20
Outputs:
- filtered: float32 [128, 512, 512], P(('frames', 'date'), 'row'), parts along dimension 0
- change: float32 [128, 512, 512], P(('frames', 'date'), 'row'), parts along dimension 0
There are 2 independent parts, one for each index of `frames`. A program takes and returns all parts, laid end to end along the dimension named above; each array names one. Nothing has to cross between parts.
All inputs are finite; a program needn't handle non-finite values.
Results may differ from a plain program's by a relative error of at most 0.00002.
Values sent between devices are 32-bit elements; how exact they have to be, the bound alone decides.
No kernel may reach another device: no remote copies, remote signals or barrier semaphores. Data moves between devices by JAX's collectives and lax.ppermute only.
A program may use at most 64 MiB of HBM per device.

v0:
```python
import jax
import jax.numpy as jnp
from jax import lax
from jax.sharding import PartitionSpec as P

RADIUS = 3


def padded_2(cells, sides, width):
    for axis, dim in sides:
        count = lax.axis_size(axis)
        ends = count - 1
        head = lax.slice_in_dim(cells, 0, width, axis=dim)
        tail = lax.slice_in_dim(cells, cells.shape[dim] - width, cells.shape[dim], axis=dim)
        cells = jnp.concatenate(
            [
                lax.ppermute(tail, axis, [(i, (i + 1) % count) for i in range(ends)]),
                cells,
                lax.ppermute(head, axis, [((i + 1) % count, i) for i in range(ends)]),
            ],
            axis=dim,
        )
    return cells


def shifted(block, axis, distance):
    devices = range(lax.axis_size(axis))
    route = [(i - distance, i) for i in devices if i - distance in devices]
    return lax.ppermute(block, axis, route)


def rim_sum(haloed, rows_n):
    width = 2 * RADIUS + 1
    cols_n = haloed.shape[2]
    padded = jnp.pad(haloed, ((0, 0), (0, 0), (RADIUS, RADIUS)))
    across = padded[:, 0:rows_n, :]
    for offset in range(1, width):
        across = across + padded[:, offset : offset + rows_n, :]
    total = across[:, :, 0:cols_n]
    for offset in range(1, width):
        total = total + across[:, :, offset : offset + cols_n]
    return total


def valid_count(first, length, extent):
    places = first + jnp.arange(length, dtype=jnp.int32)
    counted = jnp.zeros((length,), jnp.float32)
    for offset in range(-RADIUS, RADIUS + 1):
        inside = (places + offset >= 0) & (places + offset < extent)
        counted = counted + inside.astype(jnp.float32)
    return counted


def on_device(intensity):
    rows_n = intensity.shape[1]
    cols_n = intensity.shape[2]
    row_groups = lax.axis_size("row")
    date_groups = lax.axis_size("date")
    total_dates = intensity.shape[0] * date_groups
    row_first = lax.axis_index("row") * rows_n
    row_count = valid_count(row_first, rows_n, rows_n * row_groups)
    col_count = valid_count(jnp.int32(0), cols_n, cols_n)
    count = row_count[:, None] * col_count[None, :]
    haloed = padded_2(intensity, (("row", 1),), RADIUS)
    local_mean = rim_sum(haloed, rows_n) / count[None]
    is_last = lax.axis_index("date") == date_groups - 1
    ratio_sum = lax.psum(jnp.sum(intensity / local_mean, axis=0), "date")
    scale = ratio_sum[None] / jnp.float32(total_dates)
    filtered = local_mean * scale
    following = shifted(haloed[0:1], "date", -1)
    follow_mean = rim_sum(following, rows_n) / count[None]
    successor = jnp.where(is_last, filtered[-1:], follow_mean * scale)
    logged = jnp.log(filtered)
    ahead = jnp.concatenate([logged[1:], jnp.log(successor)], axis=0)
    change = ahead - logged
    return (filtered, change)


def solution(mesh):
    return jax.shard_map(
        on_device,
        mesh=mesh,
        in_specs=(P(("frames", "date"), "row", None),),
        out_specs=(P(("frames", "date"), "row", None), P(("frames", "date"), "row", None)),
        check_vma=False,
    )
```

profile of v0, /device:TPU:0, one launch (start us, length us, event | category | flops | bytes accessed | tf_op | source)
XLA Modules:
  0.0 132.5 jit_solution(6093644278905989527)
XLA Ops:
  7.2 0.0 all-reduce.4.cloned.1.call-start
  7.2 1.0 fusion.42
  8.2 2.4 %collective-permute-start = (f32[8,3,512]{2,1,0:T(4,128)S(1)}, f32[8,3,512]{2,1,0:T(4,128)S(1)}, u32[]{:S(2)}, u32[]{:S(2)}) collective-permute-start(f32[8,3,512]{2,1,0:T(4,128)S(1)} %get-tuple-element.6), channel_id=1, source_target_pairs={{0,1},{2,3},{4,5},{6,7},{8,9},{10,11},{12,13},{14,15},{16,17},{18,... | collective-permute-start | bytes 147464 | tf_op jit(solution)/shard_map/ppermute | solution.py:17
  10.6 1.3 collective-permute-start.1
  12.0 0.1 broadcast_multiply_fusion.1
  12.1 0.0 collective-permute-done
  12.1 1.7 %collective-permute-done.1 = f32[8,3,512]{2,1,0:T(4,128)S(1)} collective-permute-done((f32[8,3,512]{2,1,0:T(4,128)S(1)}, f32[8,3,512]{2,1,0:T(4,128)S(1)}, u32[]{:S(2)}, u32[]{:S(2)}) %collective-permute-start.1) | collective-permute-done | bytes 49184 | tf_op jit(solution)/shard_map/ppermute | solution.py:19
  13.8 2.8 %pad_maximum_fusion = f32[8,262,512]{2,1,0:T(8,128)S(1)} fusion(f32[8,3,512]{2,1,0:T(4,128)S(1)} %collective-permute-done.1, f32[8,256,512]{2,1,0:T(8,128)} %param.1, f32[8,3,512]{2,1,0:T(4,128)S(1)} %collective-permute-done), kind=kLoop, calls=%fused_computation.13 | loop fusion | flops 2146304 | bytes 8585216 | tf_op jit(solution)/shard_map/concatenate | solution.py:15
  16.5 0.0 copy-start
  16.5 11.3 %fusion.5 = f32[8,256,518]{2,1,0:T(8,128)S(1)} fusion(f32[8,262,512]{2,1,0:T(8,128)S(1)} %pad_maximum_fusion), kind=kLoop, calls=%fused_computation.12 | loop fusion | flops 6365184 | bytes 8536064 | tf_op jit(solution)/shard_map/add | solution.py:38
  27.9 0.0 copy-done
  27.9 10.4 %fusion.6 = (f32[256,512]{1,0:T(8,128)}, f32[8,256,512]{2,1,0:T(8,128)}) fusion(f32[8,256,512]{2,1,0:T(8,128)} %param.1, f32[256,512]{1,0:T(8,128)S(1)} %broadcast_multiply_fusion.1, f32[8,256,518]{2,1,0:T(8,128)S(1)} %fusion.5), kind=kLoop, calls=%fused_computation.23 | loop fusion | flops 9306112 | bytes 38797312 | tf_op jit(solution)/shard_map/reduce_sum | solution.py:67
  38.3 0.0 all-reduce.4.cloned.1.call-update
  38.3 1.1 slice.141
  39.4 1.5 %collective-permute-start.2 = (f32[1,262,512]{2,1,0:T(8,128)S(1)}, f32[1,262,512]{2,1,0:T(8,128)S(1)}, u32[]{:S(2)}, u32[]{:S(2)}) collective-permute-start(f32[1,262,512]{2,1,0:T(8,128)S(1)} %slice.141), channel_id=1, source_target_pairs={{2,0},{4,2},{6,4},{8,6},{10,8},{12,10},{14,12},{3,1},{5,3},{7,5},{... | collective-permute-start | bytes 1609736 | tf_op jit(solution)/shard_map/ppermute | solution.py:29
  40.9 74.4 %all-reduce.4.cloned.1.call-done = f32[256,512]{1,0:T(8,128)} async-done(((f32[256,512]{1,0:T(8,128)}), f32[256,512]{1,0:T(8,128)}) %all-reduce.4.cloned.1.call-update) | async-done | bytes 524304 | tf_op jit(solution)/shard_map/psum | solution.py:67
  115.3 1.1 broadcast_multiply_fusion
  116.4 3.3 %fusion.41 = (f32[8,256,512]{2,1,0:T(8,128)S(1)}, f32[8,256,512]{2,1,0:T(8,128)S(1)}) fusion(f32[256,512]{1,0:T(8,128)S(1)} %broadcast_multiply_fusion, f32[8,256,512]{2,1,0:T(8,128)} %get-tuple-element.5, f32[256,512]{1,0:T(8,128)S(1)} %broadcast_multiply_fusion.1), kind=kLoop, calls=%fused_computation.88 | loop fusion | flops 2097152 | bytes 13631488 | tf_op jit(solution)/shard_map/log | solution.py:73
  119.7 0.0 copy-start.1
  119.7 0.0 copy-start.2
  119.7 0.5 slice.139
  120.3 0.0 collective-permute-done.2
  120.3 1.4 %fusion.12 = f32[1,256,518]{2,1,0:T(8,128)S(1)} fusion(f32[1,262,512]{2,1,0:T(8,128)S(1)} %collective-permute-done.2), kind=kLoop, calls=%fused_computation.36 | loop fusion | flops 795648 | bytes 1067008 | tf_op jit(solution)/shard_map/add | solution.py:38
  121.7 0.0 copy-done.2
  121.7 0.9 fusion.16
  122.6 0.0 copy-done.1
  122.6 3.0 %maximum_subtract_fusion = f32[8,256,512]{2,1,0:T(8,128)} fusion(f32[1,256,512]{2,1,0:T(8,128)S(1)} %fusion.16, f32[7,256,512]{2,1,0:T(8,128)S(1)} %slice.139, f32[8,256,512]{2,1,0:T(8,128)S(1)} %get-tuple-element.3), kind=kLoop, calls=%fused_computation.20 | loop fusion | flops 2097152 | bytes 12582912 | tf_op jit(solution)/shard_map/sub | solution.py:75
  (2 shorter events, 0.0 us)
Async XLA Ops:
  7.2 108.1 %all-reduce.4.cloned.1.call-start = ((), (), s32[]{:S(2)}) async-start(), calls=%async_computation | async-start | bytes 1048576 | tf_op jit(solution)/shard_map/psum | solution.py:67
  8.2 3.9 %collective-permute-start = (f32[8,3,512]{2,1,0:T(4,128)S(1)}, f32[8,3,512]{2,1,0:T(4,128)S(1)}, u32[]{:S(2)}, u32[]{:S(2)}) collective-permute-start(f32[8,3,512]{2,1,0:T(4,128)S(1)} %get-tuple-element.6), channel_id=1, source_target_pairs={{0,1},{2,3},{4,5},{6,7},{8,9},{10,11},{12,13},{14,15},{16,17},{18,... | collective-permute-start | bytes 147464 | tf_op jit(solution)/shard_map/ppermute | solution.py:17
  10.6 3.1 %collective-permute-start.1 = (f32[8,3,512]{2,1,0:T(4,128)S(1)}, f32[8,3,512]{2,1,0:T(4,128)S(1)}, u32[]{:S(2)}, u32[]{:S(2)}) collective-permute-start(f32[8,3,512]{2,1,0:T(4,128)S(1)} %get-tuple-element.7), channel_id=1, source_target_pairs={{1,0},{3,2},{5,4},{7,6},{9,8},{11,10},{13,12},{15,14},{17,16},{19,... | collective-permute-start | bytes 147464 | tf_op jit(solution)/shard_map/ppermute | solution.py:19
  16.5 11.3 %copy-start = (f32[8,262,512]{2,1,0:T(8,128)}, f32[8,262,512]{2,1,0:T(8,128)S(1)}, u32[]{:S(2)}) copy-start(f32[8,262,512]{2,1,0:T(8,128)S(1)} %pad_maximum_fusion) | copy-start | bytes 12877828
  39.4 80.9 %collective-permute-start.2 = (f32[1,262,512]{2,1,0:T(8,128)S(1)}, f32[1,262,512]{2,1,0:T(8,128)S(1)}, u32[]{:S(2)}, u32[]{:S(2)}) collective-permute-start(f32[1,262,512]{2,1,0:T(8,128)S(1)} %slice.141), channel_id=1, source_target_pairs={{2,0},{4,2},{6,4},{8,6},{10,8},{12,10},{14,12},{3,1},{5,3},{7,5},{... | collective-permute-start | bytes 1609736 | tf_op jit(solution)/shard_map/ppermute | solution.py:29
  119.7 3.0 %copy-start.1 = (f32[8,256,512]{2,1,0:T(8,128)}, f32[8,256,512]{2,1,0:T(8,128)S(1)}, u32[]{:S(2)}) copy-start(f32[8,256,512]{2,1,0:T(8,128)S(1)} %get-tuple-element.3) | copy-start | bytes 12582916
  119.7 2.0 %copy-start.2 = (f32[256,512]{1,0:T(8,128)S(1)}, f32[256,512]{1,0:T(8,128)}, u32[]{:S(2)}) copy-start(f32[256,512]{1,0:T(8,128)} %all-reduce.4.cloned.1.call-done) | copy-start | bytes 1572868
Sparse Core Ops, SparseCore 0:
  38.4 76.8 all-reduce.3
where the time goes:
time: 133 us
  waiting for transfers between devices  76.1 us (57%)
  other arithmetic  34.4 us (26%)
  between operations  14.2 us (11%)
  starting transfers between devices  5.2 us (4%)
  local copies, waits for them, and re-layouts  2.64 us (2%)
    psum x1, waiting for transfers between devices, on_device(): ratio_sum = lax.psum(jnp.sum(intensity / local_mean, axis=0), 'date')  74.4 us
    add x2, other arithmetic, rim_sum(): across = across + padded[:, offset:offset + rows_n, :]  12.7 us
    reduce_sum x1, other arithmetic, on_device(): ratio_sum = lax.psum(jnp.sum(intensity / local_mean, axis=0), 'date')  10.4 us
    log x1, other arithmetic, on_device(): logged = jnp.log(filtered)  3.32 us
    sub x1, other arithmetic, on_device(): change = ahead - logged  3.05 us
    concatenate x1, other arithmetic, padded_2(): jnp.concatenate([lax.ppermute(tail, axis, [(i, (i + 1) % count) for i in...  2.75 us
  transfers between devices with their start and end apart: 4, of which 2 were waited for; matrix products, arithmetic and copies ran while one was open for 5% of the time, Pallas kernels for 0%

commit v1 on v0

v1 whole, which is shorter than its diff:
```python
import functools

import jax
import jax.numpy as jnp
from jax import lax
from jax.experimental import pallas as pl
from jax.experimental.pallas import tpu as pltpu
from jax.sharding import PartitionSpec as P

RADIUS = 3
LANES = 128
SUBLANES = 8
MIB = 1 << 20


def count_1d(places, extent):
    below = jnp.minimum(places, RADIUS)
    above = jnp.minimum(extent - 1 - places, RADIUS)
    return (below + above + 1).astype(jnp.float32)


def cell_count(row, col, rows_total, cols_total):
    shape = (SUBLANES, LANES)
    rows = row + lax.broadcasted_iota(jnp.int32, shape, 0)
    cols = col + lax.broadcasted_iota(jnp.int32, shape, 1)
    return count_1d(rows, rows_total) * count_1d(cols, cols_total)


def lane_shift(tiles, distance):
    lane = lax.broadcasted_iota(jnp.int32, tiles[0].shape, 1)
    zero = jnp.zeros_like(tiles[0])
    turned = [pltpu.roll(tile, (-distance) % LANES, 1) for tile in tiles]
    if distance > 0:
        beside = turned[1:] + [zero]
        own = lane < LANES - distance
    else:
        beside = [zero] + turned[:-1]
        own = lane >= -distance
    return [jnp.where(own, a, b) for a, b in zip(turned, beside)]


def window_tiles(load, tiles_n):
    across = []
    for j in range(tiles_n):
        x = [load(j, k) for k in range(-RADIUS, RADIUS + 1)]
        across.append(((x[0] + x[1]) + (x[2] + x[3])) + ((x[4] + x[5]) + x[6]))
    after = lane_shift(across, 1)
    left = [a + b for a, b in zip(lane_shift(across, -1), across)]
    right = [a + b for a, b in zip(across, after)]
    far_left = lane_shift(left, -2)
    far_right = lane_shift(right, 2)
    return [(far_left[j] + left[j]) + (after[j] + far_right[j]) for j in range(tiles_n)]


def window_kernel(parts_n, rows_total, place, image, above, below, sums, first, *rest):
    parts, (held, sem) = rest[:parts_n], rest[parts_n:]
    dates_n, rows_n, cols_n = image.shape
    tiles_n = cols_n // LANES
    part_rows = rows_n // parts_n
    me, row_first, has_above, has_below = place[0], place[1], place[2], place[3]
    copies = []
    for j in range(tiles_n):
        lanes = pl.ds(j * LANES, LANES)
        copy = pltpu.make_async_copy(
            image.at[:, :, lanes], held.at[:, j, pl.ds(SUBLANES, rows_n), :], sem.at[j]
        )
        copy.start()
        copies.append(copy)
    keep_above = (has_above > 0).astype(jnp.float32)
    keep_below = (has_below > 0).astype(jnp.float32)
    for t in range(dates_n):
        for j in range(tiles_n):
            lanes = pl.ds(j * LANES, LANES)
            held[t, j, SUBLANES - RADIUS : SUBLANES, :] = above[t, :, lanes] * keep_above
            held[t, j, SUBLANES + rows_n : SUBLANES + rows_n + RADIUS, :] = below[t, :, lanes] * keep_below
    for copy in copies:
        copy.wait()
    for k in range(parts_n):
        base = (me ^ k) * part_rows

        @pl.loop(0, part_rows // SUBLANES)
        def _(step):
            inside = pl.multiple_of(step * SUBLANES, SUBLANES)
            row = pl.multiple_of(base + inside, SUBLANES)
            ratio = [jnp.zeros((SUBLANES, LANES), jnp.float32)] * tiles_n
            for t in range(dates_n):
                total = window_tiles(
                    lambda j, d: held[t, j, pl.ds(row + SUBLANES + d, SUBLANES), :], tiles_n
                )
                for j in range(tiles_n):
                    sums[t, j, pl.ds(row, SUBLANES), :] = total[j]
                    if t == 0:
                        first[j, pl.ds(row, SUBLANES), :] = total[j]
                    ratio[j] = ratio[j] + held[t, j, pl.ds(row + SUBLANES, SUBLANES), :] / total[j]
            for j in range(tiles_n):
                count = cell_count(row_first + row, j * LANES, rows_total, cols_n)
                parts[k][pl.ds(inside, SUBLANES), pl.ds(j * LANES, LANES)] = ratio[j] * count


def window_call(image, above, below, place, parts_n, rows_total):
    dates_n, rows_n, cols_n = image.shape
    tiles_n = cols_n // LANES
    f32 = jnp.float32
    vmem = pl.BlockSpec(memory_space=pltpu.VMEM)
    out = pl.pallas_call(
        functools.partial(window_kernel, parts_n, rows_total),
        out_shape=[
            jax.ShapeDtypeStruct((dates_n, tiles_n, rows_n, LANES), f32),
            jax.ShapeDtypeStruct((tiles_n, rows_n, LANES), f32),
        ]
        + [jax.ShapeDtypeStruct((rows_n // parts_n, cols_n), f32)] * parts_n,
        in_specs=[
            pl.BlockSpec(memory_space=pltpu.SMEM),
            pl.BlockSpec(memory_space=pltpu.HBM),
            vmem,
            vmem,
        ],
        out_specs=[vmem] * (2 + parts_n),
        scratch_shapes=[
            pltpu.VMEM((dates_n, tiles_n, rows_n + 2 * SUBLANES, LANES), f32),
            pltpu.SemaphoreType.DMA((tiles_n,)),
        ],
        compiler_params=pltpu.CompilerParams(vmem_limit_bytes=24 * MIB),
        cost_estimate=pl.CostEstimate(flops=30 * image.size, bytes_accessed=8 * image.size, transcendentals=0),
        name="window",
    )(place, pltpu.with_memory_space_constraint(image, pltpu.HBM), above, below)
    return out[0], out[1], out[2:]


def change_kernel(dates_n, place, sums, after, change, ahead):
    step = pl.program_id(0)
    tiles_n = sums.shape[1]

    for j in range(tiles_n):
        lanes = pl.ds(j * LANES, LANES)
        logs = [jnp.log(sums[t, j]) for t in range(dates_n)]
        for t in range(dates_n - 1):
            change[t, :, lanes] = logs[t + 1] - logs[t]
        last = jnp.log(after[j]) - logs[dates_n - 1]
        change[dates_n - 1, :, lanes] = jnp.where(place[0] > 0, jnp.zeros_like(last), last)


def change_call(sums, after, is_last, block):
    dates_n, tiles_n, rows_n, _ = sums.shape
    cols_n = tiles_n * LANES
    return pl.pallas_call(
        functools.partial(change_kernel, dates_n),
        grid=(rows_n // block,),
        out_shape=jax.ShapeDtypeStruct((dates_n, rows_n, cols_n), jnp.float32),
        in_specs=[
            pl.BlockSpec(memory_space=pltpu.SMEM),
            pl.BlockSpec((dates_n, tiles_n, block, LANES), lambda i: (0, 0, i, 0)),
            pl.BlockSpec((tiles_n, block, LANES), lambda i: (0, i, 0)),
        ],
        out_specs=pl.BlockSpec((dates_n, block, cols_n), lambda i: (0, i, 0)),
        scratch_shapes=[pltpu.VMEM((SUBLANES, LANES), jnp.float32)],
        compiler_params=pltpu.CompilerParams(vmem_limit_bytes=16 * MIB),
        cost_estimate=pl.CostEstimate(flops=10 * sums.size, bytes_accessed=8 * sums.size, transcendentals=sums.size),
        name="change",
    )(is_last, sums, after)


def scale_kernel(parts_n, rows_total, dates_total, place, sums, *rest):
    totals, filtered = rest[:parts_n], rest[parts_n]
    dates_n, tiles_n, block, _ = sums.shape
    cols_n = tiles_n * LANES
    step = pl.program_id(0)
    for k in range(parts_n):

        @pl.when(step == k)
        def _():
            base = place[1] + (place[0] ^ k) * block

            @pl.loop(0, block // SUBLANES)
            def _(i):
                row = pl.multiple_of(i * SUBLANES, SUBLANES)
                for j in range(tiles_n):
                    lanes = pl.ds(j * LANES, LANES)
                    count = cell_count(base + row, j * LANES, rows_total, cols_n)
                    scale = totals[k][pl.ds(row, SUBLANES), lanes] / (count * dates_total)
                    for t in range(dates_n):
                        filtered[t, pl.ds(row, SUBLANES), lanes] = sums[t, j, pl.ds(row, SUBLANES), :] * scale


def scale_call(sums, totals, place, rows_total, dates_total):
    dates_n, tiles_n, rows_n, _ = sums.shape
    cols_n = tiles_n * LANES
    parts_n = len(totals)
    block = rows_n // parts_n
    return pl.pallas_call(
        functools.partial(scale_kernel, parts_n, rows_total, float(dates_total)),
        grid_spec=pltpu.PrefetchScalarGridSpec(
            num_scalar_prefetch=1,
            grid=(parts_n,),
            in_specs=[pl.BlockSpec((dates_n, tiles_n, block, LANES), lambda i, place: (0, 0, i ^ place[0], 0))]
            + [pl.BlockSpec(memory_space=pltpu.VMEM)] * parts_n,
            out_specs=pl.BlockSpec((dates_n, block, cols_n), lambda i, place: (0, i ^ place[0], 0)),
        ),
        out_shape=jax.ShapeDtypeStruct((dates_n, rows_n, cols_n), jnp.float32),
        compiler_params=pltpu.CompilerParams(vmem_limit_bytes=16 * MIB),
        cost_estimate=pl.CostEstimate(flops=2 * sums.size, bytes_accessed=8 * sums.size, transcendentals=0),
        name="scale",
    )(place, sums, *totals)


def crossed(block, axis, bits):
    return lax.ppermute(block, axis, [(i, i ^ bits) for i in range(lax.axis_size(axis))])


def halo_rows(image, axis):
    count = lax.axis_size(axis)
    index = lax.axis_index(axis)
    head = image[:, :RADIUS]
    tail = image[:, image.shape[1] - RADIUS :]
    if count == 2:
        other = lax.ppermute(jnp.where(index == 0, tail, head), axis, [(0, 1), (1, 0)])
        return other, other
    above = lax.ppermute(tail, axis, [(i, i + 1) for i in range(count - 1)])
    below = lax.ppermute(head, axis, [(i + 1, i) for i in range(count - 1)])
    return above, below


def parts_of(group, rows_n):
    if group & (group - 1):
        return 1
    parts = min(4, group)
    return parts if rows_n % (parts * SUBLANES) == 0 else 1


def on_device(image):
    dates_n, rows_n, cols_n = image.shape
    row_groups, date_groups = lax.axis_size("row"), lax.axis_size("date")
    row_index, date_index = lax.axis_index("row"), lax.axis_index("date")
    rows_total = rows_n * row_groups
    dates_total = dates_n * date_groups
    parts_n = parts_of(date_groups, rows_n)

    above, below = halo_rows(image, "row")
    place = jnp.stack(
        [
            date_index % parts_n,
            row_index * rows_n,
            (row_index > 0).astype(jnp.int32),
            (row_index < row_groups - 1).astype(jnp.int32),
        ]
    ).astype(jnp.int32)
    sums, first, parts = window_call(image, above, below, place, parts_n, rows_total)

    if parts_n == 1:
        totals = [lax.psum(parts[0], "date")]
    else:
        total = parts[0]
        for k in range(1, parts_n):
            total = total + crossed(parts[k], "date", k)
        bits = parts_n
        while bits < date_groups:
            total = total + crossed(total, "date", bits)
            bits *= 2
        totals = [total] + [crossed(total, "date", k) for k in range(1, parts_n)]

    after = lax.ppermute(first, "date", [(i + 1, i) for i in range(date_groups - 1)])
    is_last = (date_index == date_groups - 1).astype(jnp.int32).reshape(1)
    change = change_call(sums, after, is_last, min(rows_n, 32))
    filtered = scale_call(sums, totals, place, rows_total, dates_total)
    return filtered, change


def solution(mesh):
    spec = P(("frames", "date"), "row", None)
    return jax.shard_map(on_device, mesh=mesh, in_specs=(spec,), out_specs=(spec, spec), check_vma=False)
```

time: 133 us -> 63.2 us (0.48)
  waiting for transfers between devices: 76.1 us -> 25.2 us
  other arithmetic: 34.4 us -> 1.13 us
  Pallas kernels: 0 us -> 19.2 us
  between operations: 14.2 us -> 0.7 us
  starting transfers between devices: 5.2 us -> 12.6 us
  local copies, waits for them, and re-layouts: 2.64 us -> 4.2 us
    psum x1 -> x0, waiting for transfers between devices: 74.4 us -> none  [on_device(): ratio_sum = lax.psum(jnp.sum(intensity / local_mean, axis=0), 'date')]
    ppermute x3 -> x9, waiting for transfers between devices: 1.69 us -> 25.2 us  [the longest x7 24.4 us: crossed(): lax.ppermute(block, axis, [(i, i ^ bits) for i in range(lax.axis_size(axi...]
    pallas_call x0 -> x3, Pallas kernels: none -> 19.2 us  [the longest x1 11.7 us: window_call(): pl.pallas_call(functools.partial(window_kernel, parts_n, rows_total), out...]
    add x4 -> x2, other arithmetic: 12.7 us -> 0.06 us  [the longest x1 0.04 us: on_device(): total = total + crossed(parts[k], 'date', k)]
    reduce_sum x1 -> x0, other arithmetic: 10.4 us -> none  [on_device(): ratio_sum = lax.psum(jnp.sum(intensity / local_mean, axis=0), 'date')]
    ppermute x3 -> x9, starting transfers between devices: 5.16 us -> 12.6 us  [the longest x7 10.8 us: crossed(): lax.ppermute(block, axis, [(i, i ^ bits) for i in range(lax.axis_size(axi...]
    log x2 -> x0, other arithmetic: 4.25 us -> none  [the longest x1 3.32 us: on_device(): logged = jnp.log(filtered)]
    unnamed x6, local copies, waits for them, and re-layouts: 0.02 us -> 4.2 us
  transfers between devices with their start and end apart: 4 -> 9, of which waited for: 2 -> 7; matrix products, arithmetic and copies ran while one was open for 5% -> 0% of each run, Pallas kernels for 0% -> 6%
where the time goes in v1:
time: 63.2 us; the launch traced here: 63 us
  waiting for transfers between devices  25.2 us (40%)
  Pallas kernels  19.2 us (30%)
  starting transfers between devices  12.6 us (20%)
  local copies, waits for them, and re-layouts  4.2 us (7%)
  other arithmetic  1.13 us (2%)
  between operations  0.7 us (1%)
    ppermute x7, waiting for transfers between devices, crossed(): lax.ppermute(block, axis, [(i, i ^ bits) for i in range(lax.axis_size(axi...  24.4 us
    pallas_call x1, Pallas kernels, window_call(): pl.pallas_call(functools.partial(window_kernel, parts_n, rows_total), out...  11.7 us
    ppermute x7, starting transfers between devices, crossed(): lax.ppermute(block, axis, [(i, i ^ bits) for i in range(lax.axis_size(axi...  10.8 us
    unnamed x6, local copies, waits for them, and re-layouts  4.2 us
    pallas_call x1, Pallas kernels, change_call(): pl.pallas_call(functools.partial(change_kernel, dates_n), grid=(rows_n //...  3.91 us
    pallas_call x1, Pallas kernels, scale_call(): pl.pallas_call(functools.partial(scale_kernel, parts_n, rows_total, float...  3.55 us
    ppermute x1, starting transfers between devices, on_device(): lax.ppermute(first, 'date', [(i + 1, i) for i in range(date_groups - 1)])  1.28 us
  transfers between devices with their start and end apart: 9, of which 7 were waited for; matrix products, arithmetic and copies ran while one was open for 0% of the time, Pallas kernels for 6%

profile of v1, /device:TPU:0, one launch (start us, length us, event | category | flops | bytes accessed | tf_op | source)
XLA Modules:
  0.0 63.0 jit_solution(598944539865652244)
XLA Ops:
  0.6 1.0 %slice_select_fusion = f32[8,3,512]{2,1,0:T(4,128)S(1)} fusion(f32[8,256,512]{2,1,0:T(8,128)} %image.1, pred[]{:T(512)S(6)} %eq.8), kind=kLoop, calls=%fused_computation.1 | loop fusion | flops 12288 | bytes 147457 | tf_op jit(solution)/shard_map/jit(_where)/select_n | solution.py:216
  1.6 0.6 collective-permute-start
  2.2 0.1 pad_add_fusion.place
  2.3 0.8 %collective-permute-done.above.below = f32[8,3,512]{2,1,0:T(4,128)S(1)} collective-permute-done((f32[8,3,512]{2,1,0:T(4,128)S(1)}, f32[8,3,512]{2,1,0:T(4,128)S(1)}, u32[]{:S(2)}, u32[]{:S(2)}) %collective-permute-start) | collective-permute-done | bytes 49184 | tf_op jit(solution)/shard_map/ppermute | solution.py:216
  3.1 11.7 %window.1 = (f32[8,4,256,128]{3,2,1,0:T(8,128)S(1)}, f32[4,256,128]{2,1,0:T(8,128)S(1)}, f32[64,512]{1,0:T(8,128)S(1)}, f32[64,512]{1,0:T(8,128)S(1)}, f32[64,512]{1,0:T(8,128)S(1)}, /*index=5*/f32[64,512]{1,0:T(8,128)S(1)}) custom-call(s32[4]{0:T(128)S(1)} %pad_add_fusion.place, f32[8,256,512]{2,1,0:T(8,128)} %image.1, ...), custom_call_target="tpu_custom_call" | custom-call | flops 31457280 | bytes 8388608 | tf_op jit(solution)/shard_map/window/pallas_call | solution.py:105
  14.8 0.0 copy-start
  14.8 2.0 %copy-done = f32[8,4,256,128]{3,2,1,0:T(8,128)} copy-done((f32[8,4,256,128]{3,2,1,0:T(8,128)}, f32[8,4,256,128]{3,2,1,0:T(8,128)S(1)}, u32[]{:S(2)}) %copy-start) | copy-done | bytes 4194328
  16.8 2.9 %collective-permute-start.1 = (f32[64,512]{1,0:T(8,128)S(1)}, f32[64,512]{1,0:T(8,128)S(1)}, u32[]{:S(2)}, u32[]{:S(2)}) collective-permute-start(f32[64,512]{1,0:T(8,128)S(1)} %get-tuple-element.10), channel_id=1, source_target_pairs={{0,2},{2,0},{4,6},{6,4},{8,10},{10,8},{12,14},{14,12},{1,3},{3,1},... | collective-permute-start | bytes 393224 | tf_op jit(solution)/shard_map/ppermute | solution.py:207
  19.7 1.6 %collective-permute-start.2 = (f32[64,512]{1,0:T(8,128)S(1)}, f32[64,512]{1,0:T(8,128)S(1)}, u32[]{:S(2)}, u32[]{:S(2)}) collective-permute-start(f32[64,512]{1,0:T(8,128)S(1)} %get-tuple-element.11), channel_id=1, source_target_pairs={{0,4},{2,6},{4,0},{6,2},{8,12},{10,14},{12,8},{14,10},{1,5},{3,7},... | collective-permute-start | bytes 393224 | tf_op jit(solution)/shard_map/ppermute | solution.py:207
  21.3 0.0 collective-permute-start.3
  21.3 1.3 %collective-permute-start.8 = (f32[4,256,128]{2,1,0:T(8,128)S(1)}, f32[4,256,128]{2,1,0:T(8,128)S(1)}, u32[]{:S(2)}, u32[]{:S(2)}) collective-permute-start(f32[4,256,128]{2,1,0:T(8,128)S(1)} %get-tuple-element.13), channel_id=1, source_target_pairs={{2,0},{4,2},{6,4},{8,6},{10,8},{12,10},{14,12},{3,1},{5,3},{7,5},{... | collective-permute-start | bytes 1572872 | tf_op jit(solution)/shard_map/ppermute | solution.py:261
  22.5 0.9 %collective-permute-done.1 = f32[64,512]{1,0:T(8,128)S(1)} collective-permute-done((f32[64,512]{1,0:T(8,128)S(1)}, f32[64,512]{1,0:T(8,128)S(1)}, u32[]{:S(2)}, u32[]{:S(2)}) %collective-permute-start.1) | collective-permute-done | bytes 131104 | tf_op jit(solution)/shard_map/ppermute | solution.py:207
  23.5 2.6 %collective-permute-done.2 = f32[64,512]{1,0:T(8,128)S(1)} collective-permute-done((f32[64,512]{1,0:T(8,128)S(1)}, f32[64,512]{1,0:T(8,128)S(1)}, u32[]{:S(2)}, u32[]{:S(2)}) %collective-permute-start.2) | collective-permute-done | bytes 131104 | tf_op jit(solution)/shard_map/ppermute | solution.py:207
  26.0 1.6 %collective-permute-done.3 = f32[64,512]{1,0:T(8,128)S(1)} collective-permute-done((f32[64,512]{1,0:T(8,128)S(1)}, f32[64,512]{1,0:T(8,128)S(1)}, u32[]{:S(2)}, u32[]{:S(2)}) %collective-permute-start.3) | collective-permute-done | bytes 131104 | tf_op jit(solution)/shard_map/ppermute | solution.py:207
  27.7 2.8 %collective-permute-start.4 = (f32[64,512]{1,0:T(8,128)S(1)}, f32[64,512]{1,0:T(8,128)S(1)}, u32[]{:S(2)}, u32[]{:S(2)}) collective-permute-start(f32[64,512]{1,0:T(8,128)S(1)} %add_add_fusion), channel_id=1, source_target_pairs={{0,8},{2,10},{4,12},{6,14},{8,0},{10,2},{12,4},{14,6},{1,9},{3,11}... | collective-permute-start | bytes 393224 | tf_op jit(solution)/shard_map/ppermute | solution.py:207
  30.5 15.2 %collective-permute-done.4 = f32[64,512]{1,0:T(8,128)S(1)} collective-permute-done((f32[64,512]{1,0:T(8,128)S(1)}, f32[64,512]{1,0:T(8,128)S(1)}, u32[]{:S(2)}, u32[]{:S(2)}) %collective-permute-start.4) | collective-permute-done | bytes 131104 | tf_op jit(solution)/shard_map/ppermute | solution.py:207
  45.7 0.1 collective-permute-start.7
  45.8 0.1 collective-permute-start.6
  45.9 3.4 %collective-permute-start.5 = (f32[64,512]{1,0:T(8,128)S(1)}, f32[64,512]{1,0:T(8,128)S(1)}, u32[]{:S(2)}, u32[]{:S(2)}) collective-permute-start(f32[64,512]{1,0:T(8,128)S(1)} %add.20.rest_0_), channel_id=1, source_target_pairs={{0,2},{2,0},{4,6},{6,4},{8,10},{10,8},{12,14},{14,12},{1,3},{3,1},... | collective-permute-start | bytes 393224 | tf_op jit(solution)/shard_map/ppermute | solution.py:207
  49.3 2.8 %collective-permute-done.7.rest_3_ = f32[64,512]{1,0:T(8,128)S(1)} collective-permute-done((f32[64,512]{1,0:T(8,128)S(1)}, f32[64,512]{1,0:T(8,128)S(1)}, u32[]{:S(2)}, u32[]{:S(2)}) %collective-permute-start.7) | collective-permute-done | bytes 131104 | tf_op jit(solution)/shard_map/ppermute | solution.py:207
  52.1 0.0 collective-permute-done.6.rest_2_
  52.1 1.3 %collective-permute-done.5.rest_1_ = f32[64,512]{1,0:T(8,128)S(1)} collective-permute-done((f32[64,512]{1,0:T(8,128)S(1)}, f32[64,512]{1,0:T(8,128)S(1)}, u32[]{:S(2)}, u32[]{:S(2)}) %collective-permute-start.5) | collective-permute-done | bytes 131104 | tf_op jit(solution)/shard_map/ppermute | solution.py:207
  53.4 0.0 copy-start.1
  53.4 2.2 %copy-done.1 = f32[8,4,256,128]{3,2,1,0:T(8,128)S(1)} copy-done((f32[8,4,256,128]{3,2,1,0:T(8,128)S(1)}, f32[8,4,256,128]{3,2,1,0:T(8,128)}, u32[]{:S(2)}) %copy-start.1) | copy-done | bytes 4194328
  55.6 0.0 copy-start.2
  55.6 3.5 %scale.1 = f32[8,256,512]{2,1,0:T(8,128)} custom-call(s32[4]{0:T(128)S(1)} %pad_add_fusion.place, f32[8,4,256,128]{3,2,1,0:T(8,128)S(1)} %copy-done.1, f32[64,512]{1,0:T(8,128)S(1)} %add.20.rest_0_, f32[64,512]{1,0:T(8,128)S(1)} %collective-permute-done.5.rest_1_, f32[64,512]{1,0:T(8,128)S(1)} %collective-permute-done.6.rest_2_, ...), custom_call_target="tpu_custom_call" | custom-call | flops 2097152 | bytes 8388608 | tf_op jit(solution)/shard_map/scale/pallas_call | solution.py:190
  59.1 0.0 collective-permute-done.8.after
  59.1 0.0 copy-done.2
  59.1 3.9 %change.1 = f32[8,256,512]{2,1,0:T(8,128)} custom-call(s32[1]{0:T(128)} %bitcast.4.place, f32[8,4,256,128]{3,2,1,0:T(8,128)S(1)} %copy-done.2, f32[4,256,128]{2,1,0:T(8,128)S(1)} %collective-permute-done.8.after), custom_call_target="tpu_custom_call" | custom-call | flops 10485760 | bytes 8388608 | tf_op jit(solution)/shard_map/change/pallas_call | solution.py:146
  (2 shorter events, 0.1 us)
Async XLA Ops:
  1.6 1.5 %collective-permute-start = (f32[8,3,512]{2,1,0:T(4,128)S(1)}, f32[8,3,512]{2,1,0:T(4,128)S(1)}, u32[]{:S(2)}, u32[]{:S(2)}) collective-permute-start(f32[8,3,512]{2,1,0:T(4,128)S(1)} %slice_select_fusion), channel_id=1, source_target_pairs={{0,1},{1,0},{2,3},{3,2},{4,5},{5,4},{6,7},{7,6},{8,9},{9,8},{10,11... | collective-permute-start | bytes 147464 | tf_op jit(solution)/shard_map/ppermute | solution.py:216
  14.8 2.0 %copy-start = (f32[8,4,256,128]{3,2,1,0:T(8,128)}, f32[8,4,256,128]{3,2,1,0:T(8,128)S(1)}, u32[]{:S(2)}) copy-start(f32[8,4,256,128]{3,2,1,0:T(8,128)S(1)} %get-tuple-element.8.sums) | copy-start | bytes 12582916
  16.8 6.7 %collective-permute-start.1 = (f32[64,512]{1,0:T(8,128)S(1)}, f32[64,512]{1,0:T(8,128)S(1)}, u32[]{:S(2)}, u32[]{:S(2)}) collective-permute-start(f32[64,512]{1,0:T(8,128)S(1)} %get-tuple-element.10), channel_id=1, source_target_pairs={{0,2},{2,0},{4,6},{6,4},{8,10},{10,8},{12,14},{14,12},{1,3},{3,1},... | collective-permute-start | bytes 393224 | tf_op jit(solution)/shard_map/ppermute | solution.py:207
  19.7 6.4 %collective-permute-start.2 = (f32[64,512]{1,0:T(8,128)S(1)}, f32[64,512]{1,0:T(8,128)S(1)}, u32[]{:S(2)}, u32[]{:S(2)}) collective-permute-start(f32[64,512]{1,0:T(8,128)S(1)} %get-tuple-element.11), channel_id=1, source_target_pairs={{0,4},{2,6},{4,0},{6,2},{8,12},{10,14},{12,8},{14,10},{1,5},{3,7},... | collective-permute-start | bytes 393224 | tf_op jit(solution)/shard_map/ppermute | solution.py:207
  21.3 6.4 %collective-permute-start.3 = (f32[64,512]{1,0:T(8,128)S(1)}, f32[64,512]{1,0:T(8,128)S(1)}, u32[]{:S(2)}, u32[]{:S(2)}) collective-permute-start(f32[64,512]{1,0:T(8,128)S(1)} %get-tuple-element.12), channel_id=1, source_target_pairs={{0,6},{2,4},{4,2},{6,0},{8,14},{10,12},{12,10},{14,8},{1,7},{3,5},... | collective-permute-start | bytes 393224 | tf_op jit(solution)/shard_map/ppermute | solution.py:207
  21.3 37.9 %collective-permute-start.8 = (f32[4,256,128]{2,1,0:T(8,128)S(1)}, f32[4,256,128]{2,1,0:T(8,128)S(1)}, u32[]{:S(2)}, u32[]{:S(2)}) collective-permute-start(f32[4,256,128]{2,1,0:T(8,128)S(1)} %get-tuple-element.13), channel_id=1, source_target_pairs={{2,0},{4,2},{6,4},{8,6},{10,8},{12,10},{14,12},{3,1},{5,3},{7,5},{... | collective-permute-start | bytes 1572872 | tf_op jit(solution)/shard_map/ppermute | solution.py:261
  27.7 18.0 %collective-permute-start.4 = (f32[64,512]{1,0:T(8,128)S(1)}, f32[64,512]{1,0:T(8,128)S(1)}, u32[]{:S(2)}, u32[]{:S(2)}) collective-permute-start(f32[64,512]{1,0:T(8,128)S(1)} %add_add_fusion), channel_id=1, source_target_pairs={{0,8},{2,10},{4,12},{6,14},{8,0},{10,2},{12,4},{14,6},{1,9},{3,11}... | collective-permute-start | bytes 393224 | tf_op jit(solution)/shard_map/ppermute | solution.py:207
  45.7 6.4 %collective-permute-start.7 = (f32[64,512]{1,0:T(8,128)S(1)}, f32[64,512]{1,0:T(8,128)S(1)}, u32[]{:S(2)}, u32[]{:S(2)}) collective-permute-start(f32[64,512]{1,0:T(8,128)S(1)} %add.20.rest_0_), channel_id=1, source_target_pairs={{0,6},{2,4},{4,2},{6,0},{8,14},{10,12},{12,10},{14,8},{1,7},{3,5},... | collective-permute-start | bytes 393224 | tf_op jit(solution)/shard_map/ppermute | solution.py:207
  45.8 6.3 %collective-permute-start.6 = (f32[64,512]{1,0:T(8,128)S(1)}, f32[64,512]{1,0:T(8,128)S(1)}, u32[]{:S(2)}, u32[]{:S(2)}) collective-permute-start(f32[64,512]{1,0:T(8,128)S(1)} %add.20.rest_0_), channel_id=1, source_target_pairs={{0,4},{2,6},{4,0},{6,2},{8,12},{10,14},{12,8},{14,10},{1,5},{3,7},... | collective-permute-start | bytes 393224 | tf_op jit(solution)/shard_map/ppermute | solution.py:207
  45.9 7.5 %collective-permute-start.5 = (f32[64,512]{1,0:T(8,128)S(1)}, f32[64,512]{1,0:T(8,128)S(1)}, u32[]{:S(2)}, u32[]{:S(2)}) collective-permute-start(f32[64,512]{1,0:T(8,128)S(1)} %add.20.rest_0_), channel_id=1, source_target_pairs={{0,2},{2,0},{4,6},{6,4},{8,10},{10,8},{12,14},{14,12},{1,3},{3,1},... | collective-permute-start | bytes 393224 | tf_op jit(solution)/shard_map/ppermute | solution.py:207
  53.4 2.2 %copy-start.1 = (f32[8,4,256,128]{3,2,1,0:T(8,128)S(1)}, f32[8,4,256,128]{3,2,1,0:T(8,128)}, u32[]{:S(2)}) copy-start(f32[8,4,256,128]{3,2,1,0:T(8,128)} %copy-done) | copy-start | bytes 12582916
  55.6 3.6 %copy-start.2 = (f32[8,4,256,128]{3,2,1,0:T(8,128)S(1)}, f32[8,4,256,128]{3,2,1,0:T(8,128)}, u32[]{:S(2)}) copy-start(f32[8,4,256,128]{3,2,1,0:T(8,128)} %copy-done) | copy-start | bytes 12582916

commit v2 on v1

v2 whole, which is shorter than its diff:
```python
import functools

import jax
import jax.numpy as jnp
from jax import lax
from jax.experimental import pallas as pl
from jax.experimental.pallas import tpu as pltpu
from jax.sharding import PartitionSpec as P


RADIUS = 3
LANES = 128
SUBLANES = 8
MIB = 1 << 20


def count_1d(places, extent):
    below = jnp.minimum(places, RADIUS)
    above = jnp.minimum(extent - 1 - places, RADIUS)
    return (below + above + 1).astype(jnp.float32)


def cell_count(row, col, rows_total, cols_total):
    shape = (SUBLANES, LANES)
    rows = row + lax.broadcasted_iota(jnp.int32, shape, 0)
    cols = col + lax.broadcasted_iota(jnp.int32, shape, 1)
    return count_1d(rows, rows_total) * count_1d(cols, cols_total)


def lane_shift(tiles, distance):
    lane = lax.broadcasted_iota(jnp.int32, tiles[0].shape, 1)
    zero = jnp.zeros_like(tiles[0])
    turned = [pltpu.roll(tile, (-distance) % LANES, 1) for tile in tiles]
    if distance > 0:
        beside = turned[1:] + [zero]
        own = lane < LANES - distance
    else:
        beside = [zero] + turned[:-1]
        own = lane >= -distance
    return [jnp.where(own, a, b) for a, b in zip(turned, beside)]


def window_tiles(load, tiles_n):
    across = []
    for j in range(tiles_n):
        x = [load(j, k) for k in range(-RADIUS, RADIUS + 1)]
        across.append(((x[0] + x[1]) + (x[2] + x[3])) + ((x[4] + x[5]) + x[6]))
    after = lane_shift(across, 1)
    left = [a + b for a, b in zip(lane_shift(across, -1), across)]
    right = [a + b for a, b in zip(across, after)]
    far_left = lane_shift(left, -2)
    far_right = lane_shift(right, 2)
    return [(far_left[j] + left[j]) + (after[j] + far_right[j]) for j in range(tiles_n)]


def window_kernel(parts_n, rows_total, place, image, above, below, sums, *rest):
    parts, (held, ratios, sem) = rest[:parts_n], rest[parts_n:]
    dates_n, rows_n, cols_n = image.shape
    tiles_n = cols_n // LANES
    part_rows = rows_n // parts_n
    me, row_first = place[0], place[1]

    def copies(c):
        return [
            pltpu.make_async_copy(
                image.at[:, pl.ds(c * part_rows, part_rows), pl.ds(j * LANES, LANES)],
                held.at[:, j, pl.ds(SUBLANES + c * part_rows, part_rows), :],
                sem.at[c, j],
            )
            for j in range(tiles_n)
        ]

    for c in range(parts_n):
        for copy in copies(c):
            copy.start()
    fill_rims(place, held, above, below)
    for copy in copies(0):
        copy.wait()
    for c in range(parts_n):
        if c + 1 < parts_n:
            for copy in copies(c + 1):
                copy.wait()

        @pl.loop(0, part_rows // SUBLANES)
        def _(step):
            inside = pl.multiple_of(step * SUBLANES, SUBLANES)
            row = pl.multiple_of(c * part_rows + inside, SUBLANES)
            ratio = [jnp.zeros((SUBLANES, LANES), jnp.float32)] * tiles_n
            for t in range(dates_n):
                total = window_tiles(
                    lambda j, d: held[t, j, pl.ds(row + SUBLANES + d, SUBLANES), :], tiles_n
                )
                for j in range(tiles_n):
                    sums[t, j, pl.ds(row, SUBLANES), :] = total[j]
                    ratio[j] = ratio[j] + held[t, j, pl.ds(row + SUBLANES, SUBLANES), :] / total[j]
            for j in range(tiles_n):
                count = cell_count(row_first + row, j * LANES, rows_total, cols_n)
                ratios[pl.ds(inside, SUBLANES), pl.ds(j * LANES, LANES)] = ratio[j] * count

        for k in range(parts_n):

            @pl.when((me ^ k) == c)
            def _():
                parts[k][...] = ratios[...]


def fill_rims(place, held, above, below):
    dates_n, tiles_n, padded_n, _ = held.shape
    end = padded_n - SUBLANES
    keep_above = (place[2] > 0).astype(jnp.float32)
    keep_below = (place[3] > 0).astype(jnp.float32)
    for t in range(dates_n):
        for j in range(tiles_n):
            lanes = pl.ds(j * LANES, LANES)
            held[t, j, SUBLANES - RADIUS : SUBLANES, :] = above[t, :, lanes] * keep_above
            held[t, j, end : end + RADIUS, :] = below[t, :, lanes] * keep_below


def window_call(image, above, below, place, parts_n, rows_total):
    dates_n, rows_n, cols_n = image.shape
    tiles_n = cols_n // LANES
    f32 = jnp.float32
    vmem = pl.BlockSpec(memory_space=pltpu.VMEM)
    part = (rows_n // parts_n, cols_n)
    out = pl.pallas_call(
        functools.partial(window_kernel, parts_n, rows_total),
        out_shape=[jax.ShapeDtypeStruct((dates_n, tiles_n, rows_n, LANES), f32)]
        + [jax.ShapeDtypeStruct(part, f32)] * parts_n,
        in_specs=[
            pl.BlockSpec(memory_space=pltpu.SMEM),
            pl.BlockSpec(memory_space=pltpu.HBM),
            vmem,
            vmem,
        ],
        out_specs=[vmem] * (1 + parts_n),
        scratch_shapes=[
            pltpu.VMEM((dates_n, tiles_n, rows_n + 2 * SUBLANES, LANES), f32),
            pltpu.VMEM(part, f32),
            pltpu.SemaphoreType.DMA((parts_n, tiles_n)),
        ],
        compiler_params=pltpu.CompilerParams(vmem_limit_bytes=16 * MIB),
        cost_estimate=pl.CostEstimate(flops=30 * image.size, bytes_accessed=8 * image.size, transcendentals=0),
        name="window",
    )(place, pltpu.with_memory_space_constraint(image, pltpu.HBM), above, below)
    return out[0], out[1:]


def change_kernel(sums, change, held, sem):
    dates_n, tiles_n, rows_n, _ = sums.shape
    block = held.shape[2]
    copies = []
    for c in range(rows_n // block):

        @pl.loop(0, block // SUBLANES)
        def _(step):
            inside = pl.multiple_of(step * SUBLANES, SUBLANES)
            row = pl.multiple_of(c * block + inside, SUBLANES)
            for j in range(tiles_n):
                before = jnp.log(sums[0, j, pl.ds(row, SUBLANES), :])
                for t in range(dates_n - 1):
                    ahead = jnp.log(sums[t + 1, j, pl.ds(row, SUBLANES), :])
                    held[c, t, pl.ds(inside, SUBLANES), pl.ds(j * LANES, LANES)] = ahead - before
                    before = ahead

        copy = pltpu.make_async_copy(
            held.at[c], change.at[pl.ds(0, dates_n - 1), pl.ds(c * block, block), :], sem.at[c]
        )
        copy.start()
        copies.append(copy)
    for copy in copies:
        copy.wait()


def change_call(sums, block):
    dates_n, tiles_n, rows_n, _ = sums.shape
    cols_n = tiles_n * LANES
    chunks = rows_n // block
    return pl.pallas_call(
        change_kernel,
        out_shape=jax.ShapeDtypeStruct((dates_n, rows_n, cols_n), jnp.float32),
        in_specs=[pl.BlockSpec(memory_space=pltpu.VMEM)],
        out_specs=pl.BlockSpec(memory_space=pltpu.HBM),
        scratch_shapes=[
            pltpu.VMEM((chunks, dates_n - 1, block, cols_n), jnp.float32),
            pltpu.SemaphoreType.DMA((chunks,)),
        ],
        compiler_params=pltpu.CompilerParams(vmem_limit_bytes=12 * MIB),
        cost_estimate=pl.CostEstimate(flops=2000 * sums.size, bytes_accessed=8 * sums.size, transcendentals=sums.size),
        name="change",
    )(sums)


def last_kernel(unroll, place, sums, image, above, below, _, change, held, made, sem):
    dates_n, tiles_n, rows_n, _ = sums.shape
    for j in range(tiles_n):
        held[0, j, SUBLANES : SUBLANES + rows_n, :] = image[0, :, pl.ds(j * LANES, LANES)]
    fill_rims(place, held, above, below)
    keep = place[4] == 0

    @pl.loop(0, rows_n // (SUBLANES * unroll))
    def _(step):
        for u in range(unroll):
            row = pl.multiple_of((step * unroll + u) * SUBLANES, SUBLANES)
            total = window_tiles(
                lambda j, d: held[0, j, pl.ds(row + SUBLANES + d, SUBLANES), :], tiles_n
            )
            for j in range(tiles_n):
                own = sums[dates_n - 1, j, pl.ds(row, SUBLANES), :]
                ahead = jnp.where(keep, total[j], own)
                made[pl.ds(row, SUBLANES), pl.ds(j * LANES, LANES)] = jnp.log(ahead) - jnp.log(own)

    copy = pltpu.make_async_copy(made, change.at[dates_n - 1], sem)
    copy.start()
    copy.wait()


def last_call(sums, image, above, below, place, change):
    _, tiles_n, rows_n, _ = sums.shape
    cols_n = tiles_n * LANES
    whole = pl.BlockSpec(memory_space=pltpu.VMEM)
    hbm = pl.BlockSpec(memory_space=pltpu.HBM)
    unroll = 8 if rows_n % (8 * SUBLANES) == 0 else 1
    return pl.pallas_call(
        functools.partial(last_kernel, unroll),
        out_shape=jax.ShapeDtypeStruct(change.shape, jnp.float32),
        in_specs=[pl.BlockSpec(memory_space=pltpu.SMEM), whole, whole, whole, whole, hbm],
        out_specs=hbm,
        scratch_shapes=[
            pltpu.VMEM((1, tiles_n, rows_n + 2 * SUBLANES, LANES), jnp.float32),
            pltpu.VMEM((rows_n, cols_n), jnp.float32),
            pltpu.SemaphoreType.DMA,
        ],
        input_output_aliases={5: 0},
        compiler_params=pltpu.CompilerParams(vmem_limit_bytes=12 * MIB),
        cost_estimate=pl.CostEstimate(flops=2000 * image.size, bytes_accessed=12 * image.size, transcendentals=0),
        name="last",
    )(place, sums, image, above, below, change)


def scale_kernel(k, rows_total, dates_total, place, sums, total, *rest):
    filtered, held, scale, sem = rest[-4:]
    dates_n, tiles_n, _, _ = sums.shape
    cols_n = tiles_n * LANES
    block = total.shape[0]
    first = pl.multiple_of((place[0] ^ k) * block, SUBLANES)

    @pl.loop(0, block // SUBLANES)
    def _(i):
        row = pl.multiple_of(i * SUBLANES, SUBLANES)
        for j in range(tiles_n):
            lanes = pl.ds(j * LANES, LANES)
            count = cell_count(place[1] + first + row, j * LANES, rows_total, cols_n)
            scale[pl.ds(row, SUBLANES), lanes] = total[pl.ds(row, SUBLANES), lanes] / (count * dates_total)

    copies = []
    for t in range(dates_n):
        for j in range(tiles_n):
            lanes = pl.ds(j * LANES, LANES)
            held[t, :, lanes] = sums[t, j, pl.ds(first, block), :] * scale[:, lanes]
        copy = pltpu.make_async_copy(held.at[t], filtered.at[t, pl.ds(first, block), :], sem.at[t])
        copy.start()
        copies.append(copy)
    for copy in copies:
        copy.wait()


def scale_call(sums, total, place, k, rows_total, dates_total, filtered):
    dates_n, tiles_n, rows_n, _ = sums.shape
    cols_n = tiles_n * LANES
    block = total.shape[0]
    aliased = [] if filtered is None else [filtered]
    whole = pl.BlockSpec(memory_space=pltpu.VMEM)
    hbm = pl.BlockSpec(memory_space=pltpu.HBM)
    return pl.pallas_call(
        functools.partial(scale_kernel, k, rows_total, float(dates_total)),
        in_specs=[pl.BlockSpec(memory_space=pltpu.SMEM), whole, whole] + [hbm] * len(aliased),
        out_specs=hbm,
        out_shape=jax.ShapeDtypeStruct((dates_n, rows_n, cols_n), jnp.float32),
        scratch_shapes=[
            pltpu.VMEM((dates_n, block, cols_n), jnp.float32),
            pltpu.VMEM((block, cols_n), jnp.float32),
            pltpu.SemaphoreType.DMA((dates_n,)),
        ],
        input_output_aliases={3: 0} if aliased else {},
        compiler_params=pltpu.CompilerParams(vmem_limit_bytes=12 * MIB),
        cost_estimate=pl.CostEstimate(flops=500 * sums.size, bytes_accessed=8 * sums.size, transcendentals=0),
    )(place, sums, total, *aliased)


def crossed(block, axis, bits):
    return lax.ppermute(block, axis, [(i, i ^ bits) for i in range(lax.axis_size(axis))])


def halo_rows(image, axis):
    count = lax.axis_size(axis)
    index = lax.axis_index(axis)
    head = image[:, :RADIUS]
    tail = image[:, image.shape[1] - RADIUS :]
    if count == 2:
        other = lax.ppermute(jnp.where(index == 0, tail, head), axis, [(0, 1), (1, 0)])
        return other, other
    above = lax.ppermute(tail, axis, [(i, i + 1) for i in range(count - 1)])
    below = lax.ppermute(head, axis, [(i + 1, i) for i in range(count - 1)])
    return above, below


def parts_of(group, rows_n):
    if group & (group - 1):
        return 1
    parts = min(4, group)
    return parts if rows_n % (parts * SUBLANES) == 0 else 1


def on_device(image):
    dates_n, rows_n, _ = image.shape
    row_groups, date_groups = lax.axis_size("row"), lax.axis_size("date")
    row_index, date_index = lax.axis_index("row"), lax.axis_index("date")
    rows_total = rows_n * row_groups
    dates_total = dates_n * date_groups
    parts_n = parts_of(date_groups, rows_n)

    place = jnp.stack(
        [
            date_index & (parts_n - 1),
            row_index * rows_n,
            (row_index > 0).astype(jnp.int32),
            (row_index < row_groups - 1).astype(jnp.int32),
            (date_index == date_groups - 1).astype(jnp.int32),
        ]
    ).astype(jnp.int32)
    above, below = halo_rows(image, "row")
    after = lax.ppermute(image[:1], "date", [(i + 1, i) for i in range(date_groups - 1)])
    sums, parts = window_call(image, above, below, place, parts_n, rows_total)

    if parts_n == 1:
        totals = [lax.psum(parts[0], "date")]
    else:
        total = parts[0]
        for k in range(1, parts_n):
            total = total + crossed(parts[k], "date", k)
        bits = parts_n
        while bits < date_groups:
            total = total + crossed(total, "date", bits)
            bits *= 2
        totals = [total]
        for k in range(1, parts_n):
            totals.append(crossed(total, "date", k))

    change = change_call(sums, min(rows_n, 64))
    after_above, after_below = halo_rows(after, "row")
    change = last_call(sums, after, after_above, after_below, place, change)
    filtered = None
    for k in range(parts_n):
        filtered = scale_call(sums, totals[k], place, k, rows_total, dates_total, filtered)
    return filtered, change


def solution(mesh):
    spec = P(("frames", "date"), "row", None)
    return jax.shard_map(on_device, mesh=mesh, in_specs=(spec,), out_specs=(spec, spec), check_vma=False)
```

time: 63.2 us -> 58.7 us (0.929)
  waiting for transfers between devices: 25.2 us -> 19.9 us
  Pallas kernels: 19.2 us -> 22.8 us
  local copies, waits for them, and re-layouts: 4.2 us -> 1.16 us
    ppermute x7, waiting for transfers between devices: 24.4 us -> 19.1 us  [crossed(): lax.ppermute(block, axis, [(i, i ^ bits) for i in range(lax.axis_size(axi...]
    unnamed x6 -> x0, local copies, waits for them, and re-layouts: 4.2 us -> none
    pallas_call x2 -> x6, Pallas kernels: 7.46 us -> 11.6 us  [the longest x4 7.04 us: scale_call(): pl.pallas_call(functools.partial(scale_kernel, k, rows_total, float(dates...]
    slice x0 -> x1, local copies, waits for them, and re-layouts: none -> 1.08 us  [on_device(): image[:1]]
  transfers between devices with their start and end apart: 9 -> 10, of which waited for: 7 -> 4; matrix products, arithmetic and copies ran while one was open for 0% -> 2% of each run, Pallas kernels for 6% -> 16%
where the time goes in v2:
time: 58.7 us; the launch traced here: 58.5 us
  Pallas kernels  22.8 us (39%)
  waiting for transfers between devices  19.9 us (34%)
  starting transfers between devices  12.8 us (22%)
  local copies, waits for them, and re-layouts  1.16 us (2%)
  other arithmetic  1.05 us (2%)
  between operations  0.79 us (1%)
    ppermute x7, waiting for transfers between devices, crossed(): lax.ppermute(block, axis, [(i, i ^ bits) for i in range(lax.axis_size(axi...  19.1 us
    pallas_call x1, Pallas kernels, window_call(): pl.pallas_call(functools.partial(window_kernel, parts_n, rows_total), out...  11.2 us
    ppermute x7, starting transfers between devices, crossed(): lax.ppermute(block, axis, [(i, i ^ bits) for i in range(lax.axis_size(axi...  10.9 us
    pallas_call x4, Pallas kernels, scale_call(): pl.pallas_call(functools.partial(scale_kernel, k, rows_total, float(dates...  7.04 us
    pallas_call x1, Pallas kernels, last_call(): pl.pallas_call(functools.partial(last_kernel, unroll), out_shape=jax.Shap...  2.49 us
    pallas_call x1, Pallas kernels, change_call(): pl.pallas_call(change_kernel, out_shape=jax.ShapeDtypeStruct((dates_n, ro...  2.08 us
    ppermute x1, starting transfers between devices, on_device(): lax.ppermute(image[:1], 'date', [(i + 1, i) for i in range(date_groups -...  1.29 us
  transfers between devices with their start and end apart: 10, of which 4 were waited for; matrix products, arithmetic and copies ran while one was open for 2% of the time, Pallas kernels for 16%

profile of v2, /device:TPU:0, one launch (start us, length us, event | category | flops | bytes accessed | tf_op | source)
XLA Modules:
  0.0 58.5 jit_solution(5485622558225187944)
XLA Ops:
  0.6 1.0 %slice_select_fusion = f32[8,3,512]{2,1,0:T(4,128)S(1)} fusion(f32[8,256,512]{2,1,0:T(8,128)} %image.1, pred[]{:T(512)S(6)} %eq.8), kind=kLoop, calls=%fused_computation.1 | loop fusion | flops 12288 | bytes 147457 | tf_op jit(solution)/shard_map/jit(_where)/select_n | solution.py:300
  1.6 0.6 collective-permute-start
  2.2 0.1 stack.35.place
  2.3 0.8 %collective-permute-done.above.below = f32[8,3,512]{2,1,0:T(4,128)S(1)} collective-permute-done((f32[8,3,512]{2,1,0:T(4,128)S(1)}, f32[8,3,512]{2,1,0:T(4,128)S(1)}, u32[]{:S(2)}, u32[]{:S(2)}) %collective-permute-start) | collective-permute-done | bytes 49184 | tf_op jit(solution)/shard_map/ppermute | solution.py:300
  3.1 11.2 %window.1 = (f32[8,4,256,128]{3,2,1,0:T(8,128)S(1)}, f32[64,512]{1,0:T(8,128)S(1)}, f32[64,512]{1,0:T(8,128)S(1)}, f32[64,512]{1,0:T(8,128)S(1)}, f32[64,512]{1,0:T(8,128)S(1)}) custom-call(s32[5]{0:T(128)S(1)} %stack.35.place, f32[8,256,512]{2,1,0:T(8,128)} %image.1, f32[8,3,512]{2,1,0:T(4,128)S(1)} %collective-permute-done.above.below, ...), custom_call_target="tpu_custom_call" | custom-call | flops 31457280 | bytes 8388608 | tf_op jit(solution)/shard_map/window/pallas_call | solution.py:125
  14.3 2.9 %collective-permute-start.1 = (f32[64,512]{1,0:T(8,128)S(1)}, f32[64,512]{1,0:T(8,128)S(1)}, u32[]{:S(2)}, u32[]{:S(2)}) collective-permute-start(f32[64,512]{1,0:T(8,128)S(1)} %get-tuple-element.9), channel_id=1, source_target_pairs={{0,2},{2,0},{4,6},{6,4},{8,10},{10,8},{12,14},{14,12},{1,3},{3,1},... | collective-permute-start | bytes 393224 | tf_op jit(solution)/shard_map/ppermute | solution.py:291
  17.2 1.6 %collective-permute-start.2 = (f32[64,512]{1,0:T(8,128)S(1)}, f32[64,512]{1,0:T(8,128)S(1)}, u32[]{:S(2)}, u32[]{:S(2)}) collective-permute-start(f32[64,512]{1,0:T(8,128)S(1)} %get-tuple-element.10), channel_id=1, source_target_pairs={{0,4},{2,6},{4,0},{6,2},{8,12},{10,14},{12,8},{14,10},{1,5},{3,7},... | collective-permute-start | bytes 393224 | tf_op jit(solution)/shard_map/ppermute | solution.py:291
  18.8 0.0 collective-permute-start.3
  18.8 1.1 %slice.17 = f32[1,256,512]{2,1,0:T(8,128)S(1)} slice(f32[8,256,512]{2,1,0:T(8,128)} %image.1), slice={[0:1], [0:256], [0:512]} | slice | bytes 1048576 | tf_op jit(solution)/shard_map/slice | solution.py:332
  19.9 1.3 %collective-permute-start.8 = (f32[1,256,512]{2,1,0:T(8,128)S(1)}, f32[1,256,512]{2,1,0:T(8,128)S(1)}, u32[]{:S(2)}, u32[]{:S(2)}) collective-permute-start(f32[1,256,512]{2,1,0:T(8,128)S(1)} %slice.17), channel_id=1, source_target_pairs={{2,0},{4,2},{6,4},{8,6},{10,8},{12,10},{14,12},{3,1},{5,3},{7,5},{... | collective-permute-start | bytes 1572872 | tf_op jit(solution)/shard_map/ppermute | solution.py:332
  21.2 0.0 collective-permute-done.1
  21.2 2.4 %collective-permute-done.2 = f32[64,512]{1,0:T(8,128)S(1)} collective-permute-done((f32[64,512]{1,0:T(8,128)S(1)}, f32[64,512]{1,0:T(8,128)S(1)}, u32[]{:S(2)}, u32[]{:S(2)}) %collective-permute-start.2) | collective-permute-done | bytes 131104 | tf_op jit(solution)/shard_map/ppermute | solution.py:291
  23.6 1.6 %collective-permute-done.3 = f32[64,512]{1,0:T(8,128)S(1)} collective-permute-done((f32[64,512]{1,0:T(8,128)S(1)}, f32[64,512]{1,0:T(8,128)S(1)}, u32[]{:S(2)}, u32[]{:S(2)}) %collective-permute-start.3) | collective-permute-done | bytes 131104 | tf_op jit(solution)/shard_map/ppermute | solution.py:291
  25.2 2.8 %collective-permute-start.4 = (f32[64,512]{1,0:T(8,128)S(1)}, f32[64,512]{1,0:T(8,128)S(1)}, u32[]{:S(2)}, u32[]{:S(2)}) collective-permute-start(f32[64,512]{1,0:T(8,128)S(1)} %add_add_fusion), channel_id=1, source_target_pairs={{0,8},{2,10},{4,12},{6,14},{8,0},{10,2},{12,4},{14,6},{1,9},{3,11}... | collective-permute-start | bytes 393224 | tf_op jit(solution)/shard_map/ppermute | solution.py:291
  28.0 15.1 %collective-permute-done.4 = f32[64,512]{1,0:T(8,128)S(1)} collective-permute-done((f32[64,512]{1,0:T(8,128)S(1)}, f32[64,512]{1,0:T(8,128)S(1)}, u32[]{:S(2)}, u32[]{:S(2)}) %collective-permute-start.4) | collective-permute-done | bytes 131104 | tf_op jit(solution)/shard_map/ppermute | solution.py:291
  43.1 0.1 collective-permute-start.7
  43.2 0.1 collective-permute-start.6
  43.3 2.1 %change.1._ = f32[8,256,512]{2,1,0:T(8,128)} custom-call(f32[8,4,256,128]{3,2,1,0:T(8,128)S(1)} %get-tuple-element.7.sums), custom_call_target="tpu_custom_call" | custom-call | flops 2097152000 | bytes 8388608 | tf_op jit(solution)/shard_map/change/pallas_call | solution.py:178
  45.4 3.5 %collective-permute-start.5 = (f32[64,512]{1,0:T(8,128)S(1)}, f32[64,512]{1,0:T(8,128)S(1)}, u32[]{:S(2)}, u32[]{:S(2)}) collective-permute-start(f32[64,512]{1,0:T(8,128)S(1)} %add.15.total), channel_id=1, source_target_pairs={{0,6},{2,4},{4,2},{6,0},{8,14},{10,12},{12,10},{14,8},{1,7},{3,5},... | collective-permute-start | bytes 393224 | tf_op jit(solution)/shard_map/ppermute | solution.py:291
  48.8 1.8 %shard_map.30.rest_0_ = f32[8,256,512]{2,1,0:T(8,128)} custom-call(s32[5]{0:T(128)S(1)} %stack.35.place, f32[8,4,256,128]{3,2,1,0:T(8,128)S(1)} %get-tuple-element.7.sums, f32[64,512]{1,0:T(8,128)S(1)} %add.15.total), custom_call_target="tpu_custom_call" | custom-call | flops 524288000 | bytes 8388608 | tf_op jit(solution)/shard_map/pallas_call | solution.py:274
  50.6 0.0 collective-permute-done.7.total
  50.6 1.8 %shard_map.31.rest_0_ = f32[8,256,512]{2,1,0:T(8,128)} custom-call(s32[5]{0:T(128)S(1)} %stack.35.place, f32[8,4,256,128]{3,2,1,0:T(8,128)S(1)} %get-tuple-element.7.sums, f32[64,512]{1,0:T(8,128)S(1)} %collective-permute-done.7.total, f32[8,256,512]{2,1,0:T(8,128)} %shard_map.30.rest_0_), custom_call_target="tpu_custom_call", output_to_operand_aliasing={{}: (3, {})} | custom-call | flops 524288000 | bytes 8388608 | tf_op jit(solution)/shard_map/pallas_call | solution.py:274
  52.4 0.0 collective-permute-done.6.total
  52.4 1.8 %shard_map.32.rest_0_ = f32[8,256,512]{2,1,0:T(8,128)} custom-call(s32[5]{0:T(128)S(1)} %stack.35.place, f32[8,4,256,128]{3,2,1,0:T(8,128)S(1)} %get-tuple-element.7.sums, f32[64,512]{1,0:T(8,128)S(1)} %collective-permute-done.6.total, f32[8,256,512]{2,1,0:T(8,128)} %shard_map.31.rest_0_), custom_call_target="tpu_custom_call", output_to_operand_aliasing={{}: (3, {})} | custom-call | flops 524288000 | bytes 8388608 | tf_op jit(solution)/shard_map/pallas_call | solution.py:274
  54.2 0.0 collective-permute-done.8.image
  54.2 0.1 collective-permute-start.9
  54.3 0.0 collective-permute-done.5.total
  54.3 1.8 %shard_map.33 = f32[8,256,512]{2,1,0:T(8,128)} custom-call(s32[5]{0:T(128)S(1)} %stack.35.place, f32[8,4,256,128]{3,2,1,0:T(8,128)S(1)} %get-tuple-element.7.sums, f32[64,512]{1,0:T(8,128)S(1)} %collective-permute-done.5.total, f32[8,256,512]{2,1,0:T(8,128)} %shard_map.32.rest_0_), custom_call_target="tpu_custom_call", output_to_operand_aliasing={{}: (3, {})} | custom-call | flops 524288000 | bytes 8388608 | tf_op jit(solution)/shard_map/pallas_call | solution.py:274
  56.0 0.0 collective-permute-done.9.above.below
  56.0 2.5 %last.1 = f32[8,256,512]{2,1,0:T(8,128)} custom-call(s32[5]{0:T(128)S(1)} %stack.35.place, f32[8,4,256,128]{3,2,1,0:T(8,128)S(1)} %get-tuple-element.7.sums, f32[1,256,512]{2,1,0:T(8,128)S(1)} %collective-permute-done.8.image, f32[1,3,512]{2,1,0:T(4,128)S(1)} %collective-permute-done.9.above.below, ...), custom_call_target="tpu_custom_call", output_to_operand_aliasing={{}: (5, {})} | custom-call | flops 262144000 | bytes 1572864 | tf_op jit(solution)/shard_map/last/pallas_call | solution.py:223
  (3 shorter events, 0.1 us)
Async XLA Ops:
  1.6 1.5 %collective-permute-start = (f32[8,3,512]{2,1,0:T(4,128)S(1)}, f32[8,3,512]{2,1,0:T(4,128)S(1)}, u32[]{:S(2)}, u32[]{:S(2)}) collective-permute-start(f32[8,3,512]{2,1,0:T(4,128)S(1)} %slice_select_fusion), channel_id=1, source_target_pairs={{0,1},{1,0},{2,3},{3,2},{4,5},{5,4},{6,7},{7,6},{8,9},{9,8},{10,11... | collective-permute-start | bytes 147464 | tf_op jit(solution)/shard_map/ppermute | solution.py:300
  14.3 6.9 %collective-permute-start.1 = (f32[64,512]{1,0:T(8,128)S(1)}, f32[64,512]{1,0:T(8,128)S(1)}, u32[]{:S(2)}, u32[]{:S(2)}) collective-permute-start(f32[64,512]{1,0:T(8,128)S(1)} %get-tuple-element.9), channel_id=1, source_target_pairs={{0,2},{2,0},{4,6},{6,4},{8,10},{10,8},{12,14},{14,12},{1,3},{3,1},... | collective-permute-start | bytes 393224 | tf_op jit(solution)/shard_map/ppermute | solution.py:291
  17.2 6.4 %collective-permute-start.2 = (f32[64,512]{1,0:T(8,128)S(1)}, f32[64,512]{1,0:T(8,128)S(1)}, u32[]{:S(2)}, u32[]{:S(2)}) collective-permute-start(f32[64,512]{1,0:T(8,128)S(1)} %get-tuple-element.10), channel_id=1, source_target_pairs={{0,4},{2,6},{4,0},{6,2},{8,12},{10,14},{12,8},{14,10},{1,5},{3,7},... | collective-permute-start | bytes 393224 | tf_op jit(solution)/shard_map/ppermute | solution.py:291
  18.8 6.4 %collective-permute-start.3 = (f32[64,512]{1,0:T(8,128)S(1)}, f32[64,512]{1,0:T(8,128)S(1)}, u32[]{:S(2)}, u32[]{:S(2)}) collective-permute-start(f32[64,512]{1,0:T(8,128)S(1)} %get-tuple-element.11), channel_id=1, source_target_pairs={{0,6},{2,4},{4,2},{6,0},{8,14},{10,12},{12,10},{14,8},{1,7},{3,5},... | collective-permute-start | bytes 393224 | tf_op jit(solution)/shard_map/ppermute | solution.py:291
  19.9 34.3 %collective-permute-start.8 = (f32[1,256,512]{2,1,0:T(8,128)S(1)}, f32[1,256,512]{2,1,0:T(8,128)S(1)}, u32[]{:S(2)}, u32[]{:S(2)}) collective-permute-start(f32[1,256,512]{2,1,0:T(8,128)S(1)} %slice.17), channel_id=1, source_target_pairs={{2,0},{4,2},{6,4},{8,6},{10,8},{12,10},{14,12},{3,1},{5,3},{7,5},{... | collective-permute-start | bytes 1572872 | tf_op jit(solution)/shard_map/ppermute | solution.py:332
  25.2 17.9 %collective-permute-start.4 = (f32[64,512]{1,0:T(8,128)S(1)}, f32[64,512]{1,0:T(8,128)S(1)}, u32[]{:S(2)}, u32[]{:S(2)}) collective-permute-start(f32[64,512]{1,0:T(8,128)S(1)} %add_add_fusion), channel_id=1, source_target_pairs={{0,8},{2,10},{4,12},{6,14},{8,0},{10,2},{12,4},{14,6},{1,9},{3,11}... | collective-permute-start | bytes 393224 | tf_op jit(solution)/shard_map/ppermute | solution.py:291
  43.1 7.5 %collective-permute-start.7 = (f32[64,512]{1,0:T(8,128)S(1)}, f32[64,512]{1,0:T(8,128)S(1)}, u32[]{:S(2)}, u32[]{:S(2)}) collective-permute-start(f32[64,512]{1,0:T(8,128)S(1)} %add.15.total), channel_id=1, source_target_pairs={{0,2},{2,0},{4,6},{6,4},{8,10},{10,8},{12,14},{14,12},{1,3},{3,1},... | collective-permute-start | bytes 393224 | tf_op jit(solution)/shard_map/ppermute | solution.py:291
  43.2 9.2 %collective-permute-start.6 = (f32[64,512]{1,0:T(8,128)S(1)}, f32[64,512]{1,0:T(8,128)S(1)}, u32[]{:S(2)}, u32[]{:S(2)}) collective-permute-start(f32[64,512]{1,0:T(8,128)S(1)} %add.15.total), channel_id=1, source_target_pairs={{0,4},{2,6},{4,0},{6,2},{8,12},{10,14},{12,8},{14,10},{1,5},{3,7},... | collective-permute-start | bytes 393224 | tf_op jit(solution)/shard_map/ppermute | solution.py:291
  45.4 8.9 %collective-permute-start.5 = (f32[64,512]{1,0:T(8,128)S(1)}, f32[64,512]{1,0:T(8,128)S(1)}, u32[]{:S(2)}, u32[]{:S(2)}) collective-permute-start(f32[64,512]{1,0:T(8,128)S(1)} %add.15.total), channel_id=1, source_target_pairs={{0,6},{2,4},{4,2},{6,0},{8,14},{10,12},{12,10},{14,8},{1,7},{3,5},... | collective-permute-start | bytes 393224 | tf_op jit(solution)/shard_map/ppermute | solution.py:291
  54.2 1.9 %collective-permute-start.9 = (f32[1,3,512]{2,1,0:T(4,128)S(1)}, f32[1,3,512]{2,1,0:T(4,128)S(1)}, u32[]{:S(2)}, u32[]{:S(2)}) collective-permute-start(f32[1,3,512]{2,1,0:T(4,128)S(1)} %slice_select_fusion.1), channel_id=1, source_target_pairs={{0,1},{1,0},{2,3},{3,2},{4,5},{5,4},{6,7},{7,6},{8,9},{9,8},{10,11... | collective-permute-start | bytes 18440 | tf_op jit(solution)/shard_map/ppermute | solution.py:300

commit v3 on v1

v3 whole, which is shorter than its diff:
```python
import functools

import jax
import jax.numpy as jnp
from jax import lax
from jax.experimental import pallas as pl
from jax.experimental.pallas import tpu as pltpu
from jax.sharding import PartitionSpec as P


RADIUS = 3
LANES = 128
SUBLANES = 8
MIB = 1 << 20


def count_1d(places, extent):
    below = jnp.minimum(places, RADIUS)
    above = jnp.minimum(extent - 1 - places, RADIUS)
    return (below + above + 1).astype(jnp.float32)


def cell_count(row, col, rows_total, cols_total):
    shape = (SUBLANES, LANES)
    rows = row + lax.broadcasted_iota(jnp.int32, shape, 0)
    cols = col + lax.broadcasted_iota(jnp.int32, shape, 1)
    return count_1d(rows, rows_total) * count_1d(cols, cols_total)


def lane_shift(tiles, distance):
    lane = lax.broadcasted_iota(jnp.int32, tiles[0].shape, 1)
    zero = jnp.zeros_like(tiles[0])
    turned = [pltpu.roll(tile, (-distance) % LANES, 1) for tile in tiles]
    if distance > 0:
        beside = turned[1:] + [zero]
        own = lane < LANES - distance
    else:
        beside = [zero] + turned[:-1]
        own = lane >= -distance
    return [jnp.where(own, a, b) for a, b in zip(turned, beside)]


def window_tiles(load, tiles_n):
    across = []
    for j in range(tiles_n):
        x = [load(j, k) for k in range(-RADIUS, RADIUS + 1)]
        across.append(((x[0] + x[1]) + (x[2] + x[3])) + ((x[4] + x[5]) + x[6]))
    after = lane_shift(across, 1)
    left = [a + b for a, b in zip(lane_shift(across, -1), across)]
    right = [a + b for a, b in zip(across, after)]
    far_left = lane_shift(left, -2)
    far_right = lane_shift(right, 2)
    return [(far_left[j] + left[j]) + (after[j] + far_right[j]) for j in range(tiles_n)]


def part_row(place, k, part_rows):
    return pl.multiple_of((place[0] ^ k) * part_rows, SUBLANES)


def window_kernel(k, rows_total, dates_total, place, image, above, below, sums, part, *rest):
    held = rest[-1]
    dates_n, rows_n, cols_n = image.shape
    tiles_n, part_rows = sums.shape[1], sums.shape[2]
    first = part_row(place, k, part_rows)
    end = SUBLANES + part_rows
    tiles = [(t, j, pl.ds(j * LANES, LANES)) for t in range(dates_n) for j in range(tiles_n)]
    for t, j, lanes in tiles:
        held[t, j, SUBLANES:end, :] = image[t, pl.ds(first, part_rows), lanes]

    @pl.when(first > 0)
    def _():
        for t, j, lanes in tiles:
            held[t, j, :SUBLANES, :] = image[t, pl.ds(pl.multiple_of(first - SUBLANES, SUBLANES), SUBLANES), lanes]

    @pl.when(first == 0)
    def _():
        fill_above(place, held, above)

    @pl.when(first + part_rows < rows_n)
    def _():
        for t, j, lanes in tiles:
            held[t, j, end:, :] = image[t, pl.ds(pl.multiple_of(first + part_rows, SUBLANES), SUBLANES), lanes]

    @pl.when(first + part_rows == rows_n)
    def _():
        fill_below(place, held, below)

    @pl.loop(0, part_rows // SUBLANES)
    def _(step):
        row = pl.multiple_of(step * SUBLANES, SUBLANES)
        ratio = [jnp.zeros((SUBLANES, LANES), jnp.float32)] * tiles_n
        for t in range(dates_n):
            total = window_tiles(
                lambda j, d: held[t, j, pl.ds(row + SUBLANES + d, SUBLANES), :], tiles_n
            )
            for j in range(tiles_n):
                sums[t, j, pl.ds(row, SUBLANES), :] = total[j]
                ratio[j] = ratio[j] + held[t, j, pl.ds(row + SUBLANES, SUBLANES), :] / total[j]
        for j in range(tiles_n):
            count = cell_count(place[1] + first + row, j * LANES, rows_total, cols_n)
            part[pl.ds(row, SUBLANES), pl.ds(j * LANES, LANES)] = ratio[j] * count
            if k == 0:
                rest[0][pl.ds(row, SUBLANES), pl.ds(j * LANES, LANES)] = 1.0 / (count * dates_total)


def fill_above(place, held, above):
    keep = (place[2] > 0).astype(jnp.float32)
    for t in range(held.shape[0]):
        for j in range(held.shape[1]):
            held[t, j, SUBLANES - RADIUS : SUBLANES, :] = above[t, :, pl.ds(j * LANES, LANES)] * keep


def fill_below(place, held, below):
    end = held.shape[2] - SUBLANES
    keep = (place[3] > 0).astype(jnp.float32)
    for t in range(held.shape[0]):
        for j in range(held.shape[1]):
            held[t, j, end : end + RADIUS, :] = below[t, :, pl.ds(j * LANES, LANES)] * keep


SCALARS = pl.BlockSpec(memory_space=pltpu.SMEM)
WHOLE = pl.BlockSpec(memory_space=pltpu.VMEM)
OUTER = pl.BlockSpec(memory_space=pltpu.HBM)


def window_call(image, above, below, place, k, parts_n, rows_total, dates_total):
    dates_n, rows_n, cols_n = image.shape
    tiles_n = cols_n // LANES
    part_rows = rows_n // parts_n
    outs = 2 if k == 0 else 1
    f32 = jnp.float32
    return pl.pallas_call(
        functools.partial(window_kernel, k, rows_total, float(dates_total)),
        out_shape=[
            jax.ShapeDtypeStruct((dates_n, tiles_n, part_rows, LANES), f32),
        ]
        + [jax.ShapeDtypeStruct((part_rows, cols_n), f32)] * outs,
        in_specs=[SCALARS, WHOLE, WHOLE, WHOLE],
        out_specs=[WHOLE] * (1 + outs),
        scratch_shapes=[pltpu.VMEM((dates_n, tiles_n, part_rows + 2 * SUBLANES, LANES), f32)],
        compiler_params=pltpu.CompilerParams(vmem_limit_bytes=12 * MIB),
        cost_estimate=pl.CostEstimate(flops=500 * image.size, bytes_accessed=8 * image.size, transcendentals=0),
    )(place, image, above, below)


def change_kernel(parts_n, place, *rest):
    sums = rest[:parts_n]
    change, held, sem = rest[parts_n:]
    dates_n, tiles_n, part_rows, _ = sums[0].shape
    copies = []
    for k in range(parts_n):

        @pl.loop(0, part_rows // SUBLANES)
        def _(step):
            rows = pl.ds(pl.multiple_of(step * SUBLANES, SUBLANES), SUBLANES)
            for j in range(tiles_n):
                before = jnp.log(sums[k][0, j, rows, :])
                for t in range(dates_n - 1):
                    ahead = jnp.log(sums[k][t + 1, j, rows, :])
                    held[k, t, rows, pl.ds(j * LANES, LANES)] = ahead - before
                    before = ahead

        place_rows = pl.ds(part_row(place, k, part_rows), part_rows)
        copy = pltpu.make_async_copy(held.at[k], change.at[pl.ds(0, dates_n - 1), place_rows, :], sem.at[k])
        copy.start()
        copies.append(copy)
    for copy in copies:
        copy.wait()


def change_call(sums, place):
    parts_n = len(sums)
    dates_n, tiles_n, part_rows, _ = sums[0].shape
    cols_n = tiles_n * LANES
    size = parts_n * sums[0].size
    return pl.pallas_call(
        functools.partial(change_kernel, parts_n),
        out_shape=jax.ShapeDtypeStruct((dates_n, parts_n * part_rows, cols_n), jnp.float32),
        in_specs=[SCALARS] + [WHOLE] * parts_n,
        out_specs=OUTER,
        scratch_shapes=[
            pltpu.VMEM((parts_n, dates_n - 1, part_rows, cols_n), jnp.float32),
            pltpu.SemaphoreType.DMA((parts_n,)),
        ],
        compiler_params=pltpu.CompilerParams(vmem_limit_bytes=12 * MIB),
        cost_estimate=pl.CostEstimate(flops=2000 * size, bytes_accessed=8 * size, transcendentals=size),
        name="change",
    )(place, *sums)


def last_kernel(parts_n, unroll, place, *rest):
    sums, pieces = rest[:parts_n], rest[parts_n:-7]
    above, below, _, change, held, made, sem = rest[-7:]
    dates_n, tiles_n, part_rows, _ = sums[0].shape
    start = SUBLANES
    for piece in pieces:
        for j in range(tiles_n):
            held[0, j, start : start + piece.shape[1], :] = piece[0, :, pl.ds(j * LANES, LANES)]
        start += piece.shape[1]
    fill_above(place, held, above)
    fill_below(place, held, below)
    keep = place[4] == 0
    for k in range(parts_n):
        first = part_row(place, k, part_rows)

        @pl.loop(0, part_rows // (SUBLANES * unroll))
        def _(step):
            for u in range(unroll):
                inside = pl.multiple_of((step * unroll + u) * SUBLANES, SUBLANES)
                row = pl.multiple_of(first + inside, SUBLANES)
                total = window_tiles(
                    lambda j, d: held[0, j, pl.ds(row + SUBLANES + d, SUBLANES), :], tiles_n
                )
                for j in range(tiles_n):
                    own = sums[k][dates_n - 1, j, pl.ds(inside, SUBLANES), :]
                    ahead = jnp.where(keep, total[j], own)
                    made[pl.ds(row, SUBLANES), pl.ds(j * LANES, LANES)] = jnp.log(ahead) - jnp.log(own)

    copy = pltpu.make_async_copy(made, change.at[dates_n - 1], sem)
    copy.start()
    copy.wait()


def last_call(sums, pieces, above, below, place, change):
    parts_n = len(sums)
    _, tiles_n, part_rows, _ = sums[0].shape
    rows_n, cols_n = parts_n * part_rows, tiles_n * LANES
    inputs = parts_n + len(pieces) + 3
    unroll = 8 if part_rows % (8 * SUBLANES) == 0 else 1
    return pl.pallas_call(
        functools.partial(last_kernel, parts_n, unroll),
        out_shape=jax.ShapeDtypeStruct(change.shape, jnp.float32),
        in_specs=[SCALARS] + [WHOLE] * (inputs - 1) + [OUTER],
        out_specs=OUTER,
        scratch_shapes=[
            pltpu.VMEM((1, tiles_n, rows_n + 2 * SUBLANES, LANES), jnp.float32),
            pltpu.VMEM((rows_n, cols_n), jnp.float32),
            pltpu.SemaphoreType.DMA,
        ],
        input_output_aliases={inputs: 0},
        compiler_params=pltpu.CompilerParams(vmem_limit_bytes=12 * MIB),
        cost_estimate=pl.CostEstimate(flops=2000 * rows_n * cols_n, bytes_accessed=12 * rows_n * cols_n, transcendentals=0),
        name="last",
    )(place, *sums, *pieces, above, below, change)


def scale_kernel(ks, place, *rest):
    n = len(ks)
    sums, scales = rest[:n], rest[n : 2 * n]
    filtered, held, sem = rest[-3:]
    dates_n, tiles_n, part_rows, _ = sums[0].shape
    copies = []
    for i, k in enumerate(ks):
        rows = pl.ds(part_row(place, k, part_rows), part_rows)
        for t in range(dates_n):
            for j in range(tiles_n):
                lanes = pl.ds(j * LANES, LANES)
                held[i, t, :, lanes] = sums[i][t, j] * scales[i][:, lanes]
            copy = pltpu.make_async_copy(held.at[i, t], filtered.at[t, rows, :], sem.at[i, t])
            copy.start()
            copies.append(copy)
    for copy in copies:
        copy.wait()


def scale_call(sums, scales, place, ks, rows_n, filtered):
    n = len(ks)
    dates_n, tiles_n, part_rows, _ = sums[0].shape
    cols_n = tiles_n * LANES
    size = n * sums[0].size
    aliased = [] if filtered is None else [filtered]
    return pl.pallas_call(
        functools.partial(scale_kernel, ks),
        in_specs=[SCALARS] + [WHOLE] * (2 * n) + [OUTER] * len(aliased),
        out_specs=OUTER,
        out_shape=jax.ShapeDtypeStruct((dates_n, rows_n, cols_n), jnp.float32),
        scratch_shapes=[
            pltpu.VMEM((n, dates_n, part_rows, cols_n), jnp.float32),
            pltpu.SemaphoreType.DMA((n, dates_n)),
        ],
        input_output_aliases={2 * n + 1: 0} if aliased else {},
        compiler_params=pltpu.CompilerParams(vmem_limit_bytes=12 * MIB),
        cost_estimate=pl.CostEstimate(flops=1000 * size, bytes_accessed=8 * size, transcendentals=0),
    )(place, *sums, *scales, *aliased)


def crossed(block, axis, bits):
    return lax.ppermute(block, axis, [(i, i ^ bits) for i in range(lax.axis_size(axis))])


def halo_rows(pieces, axis, is_first):
    count = lax.axis_size(axis)
    head = pieces[0][:, :RADIUS]
    tail = pieces[-1][:, pieces[-1].shape[1] - RADIUS :]
    if count == 2:
        other = lax.ppermute(jnp.where(is_first, tail, head), axis, [(0, 1), (1, 0)])
        return other, other
    above = lax.ppermute(tail, axis, [(i, i + 1) for i in range(count - 1)])
    below = lax.ppermute(head, axis, [(i + 1, i) for i in range(count - 1)])
    return above, below


def rim_kernel(place, first, final, rim):
    is_first = place[2] == 0
    rows_n = final.shape[1]
    tail = final[:, rows_n - SUBLANES :, :]
    head = first[:, :SUBLANES, :]
    rim[...] = jnp.where(is_first, tail[:, SUBLANES - RADIUS :, :], head[:, :RADIUS, :])


def rim_call(pieces, place):
    first, final = pieces[0], pieces[-1]
    return pl.pallas_call(
        rim_kernel,
        out_shape=jax.ShapeDtypeStruct((first.shape[0], RADIUS, first.shape[2]), jnp.float32),
        in_specs=[SCALARS, WHOLE, WHOLE],
        out_specs=WHOLE,
        compiler_params=pltpu.CompilerParams(vmem_limit_bytes=4 * MIB),
        name="rim",
    )(place, first, final)


def prepare_kernel(place, image, rim, early, held, sem):
    rows_n = image.shape[1]
    is_first = place[2] == 0
    start = pl.multiple_of(jnp.where(is_first, rows_n - SUBLANES, 0), SUBLANES)
    edge = pltpu.make_async_copy(image.at[:, pl.ds(start, SUBLANES), :], held, sem.at[0])
    edge.start()
    copy = pltpu.make_async_copy(image.at[pl.ds(0, 1), pl.ds(0, early.shape[1]), :], early, sem.at[1])
    copy.start()
    edge.wait()
    rim[...] = jnp.where(is_first, held[:, SUBLANES - RADIUS :, :], held[:, :RADIUS, :])
    copy.wait()


def prepare_call(image, place, cut):
    dates_n, _, cols_n = image.shape
    return pl.pallas_call(
        prepare_kernel,
        out_shape=[
            jax.ShapeDtypeStruct((dates_n, RADIUS, cols_n), jnp.float32),
            jax.ShapeDtypeStruct((1, cut, cols_n), jnp.float32),
        ],
        in_specs=[SCALARS, OUTER],
        out_specs=[WHOLE, WHOLE],
        scratch_shapes=[pltpu.VMEM((dates_n, SUBLANES, cols_n), jnp.float32), pltpu.SemaphoreType.DMA((2,))],
        compiler_params=pltpu.CompilerParams(vmem_limit_bytes=4 * MIB),
        name="prepare",
    )(place, pltpu.with_memory_space_constraint(image, pltpu.HBM))


def parts_of(group, rows_n):
    if group & (group - 1):
        return 1
    parts = min(4, group)
    return parts if rows_n % (parts * SUBLANES) == 0 else 1


def on_device(image):
    dates_n, rows_n, _ = image.shape
    row_groups, date_groups = lax.axis_size("row"), lax.axis_size("date")
    row_index, date_index = lax.axis_index("row"), lax.axis_index("date")
    rows_total = rows_n * row_groups
    dates_total = dates_n * date_groups
    parts_n = parts_of(date_groups, rows_n)

    place = jnp.stack(
        [
            date_index & (parts_n - 1),
            row_index * rows_n,
            (row_index > 0).astype(jnp.int32),
            (row_index < row_groups - 1).astype(jnp.int32),
            (date_index == date_groups - 1).astype(jnp.int32),
        ]
    ).astype(jnp.int32)
    cut = rows_n
    route = [(i + 1, i) for i in range(date_groups - 1)]
    if row_groups == 2:
        rim, early = prepare_call(image, place, cut)
        above = below = lax.ppermute(rim, "row", [(0, 1), (1, 0)])
    else:
        early = image[:1, :cut]
        above, below = halo_rows([image], "row", place[2] == 0)
    after = [lax.ppermute(early, "date", route)]
    if cut < rows_n:
        after.append(lax.ppermute(image[:1, cut:], "date", route))
    sums, parts = [], []
    for k in range(parts_n):
        made = window_call(image, above, below, place, k, parts_n, rows_total, dates_total)
        sums.append(made[0])
        parts.append(made[1])
        if k == 0:
            norm = made[2]

    if parts_n == 1:
        total = lax.psum(parts[0], "date")
    else:
        total = parts[0]
        for k in range(1, parts_n):
            total = total + crossed(parts[k], "date", k)
        bits = parts_n
        while bits < date_groups:
            total = total + crossed(total, "date", bits)
            bits *= 2
    scales = [total * norm]
    for k in range(1, parts_n):
        scales.append(crossed(scales[0], "date", k))

    change = change_call(sums, place)
    if row_groups == 2:
        after_above = after_below = lax.ppermute(rim_call(after, place), "row", [(0, 1), (1, 0)])
    else:
        after_above, after_below = halo_rows(after, "row", place[2] == 0)
    change = last_call(sums, after, after_above, after_below, place, change)
    filtered = scale_call(sums[:1], scales[:1], place, (0,), rows_n, None)
    if parts_n > 1:
        filtered = scale_call(sums[1:], scales[1:], place, tuple(range(1, parts_n)), rows_n, filtered)
    return filtered, change


def solution(mesh):
    spec = P(("frames", "date"), "row", None)
    return jax.shard_map(on_device, mesh=mesh, in_specs=(spec,), out_specs=(spec, spec), check_vma=False)
```

time: 63.2 us -> 51.5 us (0.81)
  waiting for transfers between devices: 25.2 us -> 13.3 us
  Pallas kernels: 19.2 us -> 24.1 us
  local copies, waits for them, and re-layouts: 4.2 us -> 0.09 us
  other arithmetic: 1.13 us -> 0.07 us
    ppermute x7, waiting for transfers between devices: 24.4 us -> 7.9 us  [crossed(): lax.ppermute(block, axis, [(i, i ^ bits) for i in range(lax.axis_size(axi...]
    pallas_call x3 -> x10, Pallas kernels: 19.2 us -> 24.1 us  [the longest x4 11.5 us: window_call(): pl.pallas_call(functools.partial(window_kernel, k, rows_total, float(date...]
    ppermute x2 -> x3, waiting for transfers between devices: 0.83 us -> 5.44 us  [the longest x1 4.53 us: on_device(): after = [lax.ppermute(early, 'date', route)]]
    unnamed x6 -> x2, local copies, waits for them, and re-layouts: 4.2 us -> 0.01 us
    select_n x1 -> x0, other arithmetic: 0.99 us -> none  [halo_rows(): jnp.where(index == 0, tail, head)]
    ppermute x2 -> x3, starting transfers between devices: 1.84 us -> 1.91 us  [the longest x1 1.28 us: on_device(): after = [lax.ppermute(early, 'date', route)]]
  transfers between devices with their start and end apart: 9 -> 10, of which waited for: 7 -> 6; matrix products, arithmetic and copies ran while one was open for 0% -> 0% of each run, Pallas kernels for 6% -> 31%
where the time goes in v3:
time: 51.5 us; the launch traced here: 51.1 us
  Pallas kernels  24.1 us (47%)
  waiting for transfers between devices  13.3 us (26%)
  starting transfers between devices  12.8 us (25%)
  between operations  0.77 us (1%)
    pallas_call x4, Pallas kernels, window_call(): pl.pallas_call(functools.partial(window_kernel, k, rows_total, float(date...  11.5 us
    ppermute x7, starting transfers between devices, crossed(): lax.ppermute(block, axis, [(i, i ^ bits) for i in range(lax.axis_size(axi...  10.8 us
    ppermute x7, waiting for transfers between devices, crossed(): lax.ppermute(block, axis, [(i, i ^ bits) for i in range(lax.axis_size(axi...  7.9 us
    ppermute x1, waiting for transfers between devices, on_device(): after = [lax.ppermute(early, 'date', route)]  4.53 us
    pallas_call x2, Pallas kernels, scale_call(): pl.pallas_call(functools.partial(scale_kernel, ks), in_specs=[SCALARS] +...  3.99 us
    pallas_call x1, Pallas kernels, last_call(): pl.pallas_call(functools.partial(last_kernel, parts_n, unroll), out_shape...  3.51 us
    pallas_call x1, Pallas kernels, change_call(): pl.pallas_call(functools.partial(change_kernel, parts_n), out_shape=jax.S...  2.62 us
    pallas_call x1, Pallas kernels, prepare_call(): pl.pallas_call(prepare_kernel, out_shape=[jax.ShapeDtypeStruct((dates_n,...  1.94 us
  transfers between devices with their start and end apart: 10, of which 6 were waited for; matrix products, arithmetic and copies ran while one was open for 0% of the time, Pallas kernels for 31%

profile of v3, /device:TPU:0, one launch (start us, length us, event | category | flops | bytes accessed | tf_op | source)
XLA Modules:
  0.0 51.1 jit_solution(642660962281206774)
XLA Ops:
  0.6 0.1 stack.35.place
  0.7 0.0 copy-start
  0.7 1.9 %prepare.1 = (f32[8,3,512]{2,1,0:T(4,128)S(1)}, f32[1,256,512]{2,1,0:T(8,128)S(1)}) custom-call(s32[5]{0:T(128)S(1)} %stack.35.place, f32[8,256,512]{2,1,0:T(8,128)} %image.9), custom_call_target="tpu_custom_call" | custom-call | tf_op jit(solution)/shard_map/prepare/pallas_call | solution.py:338
  2.7 0.6 %collective-permute-start = (f32[8,3,512]{2,1,0:T(4,128)S(1)}, f32[8,3,512]{2,1,0:T(4,128)S(1)}, u32[]{:S(2)}, u32[]{:S(2)}) collective-permute-start(f32[8,3,512]{2,1,0:T(4,128)S(1)} %get-tuple-element.13), channel_id=1, source_target_pairs={{0,1},{1,0},{2,3},{3,2},{4,5},{5,4},{6,7},{7,6},{8,9},{9,8},{10,11... | collective-permute-start | bytes 147464 | tf_op jit(solution)/shard_map/ppermute | solution.py:380
  3.2 0.9 %collective-permute-done.above.below = f32[8,3,512]{2,1,0:T(4,128)S(1)} collective-permute-done((f32[8,3,512]{2,1,0:T(4,128)S(1)}, f32[8,3,512]{2,1,0:T(4,128)S(1)}, u32[]{:S(2)}, u32[]{:S(2)}) %collective-permute-start) | collective-permute-done | bytes 49184 | tf_op jit(solution)/shard_map/ppermute | solution.py:380
  4.1 0.0 copy-done
  4.1 2.9 %shard_map.31 = (f32[8,4,64,128]{3,2,1,0:T(8,128)S(1)}, f32[64,512]{1,0:T(8,128)S(1)}) custom-call(s32[5]{0:T(128)S(1)} %stack.35.place, f32[8,256,512]{2,1,0:T(8,128)S(1)} %copy-done, f32[8,3,512]{2,1,0:T(4,128)S(1)} %collective-permute-done.above.below, f32[8,3,512]{2,1,0:T(4,128)S(1)} %collective-permute-done.above.below), custom_call_target="tpu_custom_call" | custom-call | flops 524288000 | bytes 8388608 | tf_op jit(solution)/shard_map/pallas_call | solution.py:132
  7.0 3.0 %collective-permute-start.2 = (f32[64,512]{1,0:T(8,128)S(1)}, f32[64,512]{1,0:T(8,128)S(1)}, u32[]{:S(2)}, u32[]{:S(2)}) collective-permute-start(f32[64,512]{1,0:T(8,128)S(1)} %get-tuple-element.19), channel_id=1, source_target_pairs={{0,4},{2,6},{4,0},{6,2},{8,12},{10,14},{12,8},{14,10},{1,5},{3,7},... | collective-permute-start | bytes 393224 | tf_op jit(solution)/shard_map/ppermute | solution.py:288
  10.0 2.9 %shard_map.32 = (f32[8,4,64,128]{3,2,1,0:T(8,128)S(1)}, f32[64,512]{1,0:T(8,128)S(1)}) custom-call(s32[5]{0:T(128)S(1)} %stack.35.place, f32[8,256,512]{2,1,0:T(8,128)S(1)} %copy-done, f32[8,3,512]{2,1,0:T(4,128)S(1)} %collective-permute-done.above.below, f32[8,3,512]{2,1,0:T(4,128)S(1)} %collective-permute-done.above.below), custom_call_target="tpu_custom_call" | custom-call | flops 524288000 | bytes 8388608 | tf_op jit(solution)/shard_map/pallas_call | solution.py:132
  12.9 1.5 %collective-permute-start.3 = (f32[64,512]{1,0:T(8,128)S(1)}, f32[64,512]{1,0:T(8,128)S(1)}, u32[]{:S(2)}, u32[]{:S(2)}) collective-permute-start(f32[64,512]{1,0:T(8,128)S(1)} %get-tuple-element.20), channel_id=1, source_target_pairs={{0,6},{2,4},{4,2},{6,0},{8,14},{10,12},{12,10},{14,8},{1,7},{3,5},... | collective-permute-start | bytes 393224 | tf_op jit(solution)/shard_map/ppermute | solution.py:288
  14.3 2.9 %shard_map.30 = (f32[8,4,64,128]{3,2,1,0:T(8,128)S(1)}, f32[64,512]{1,0:T(8,128)S(1)}) custom-call(s32[5]{0:T(128)S(1)} %stack.35.place, f32[8,256,512]{2,1,0:T(8,128)S(1)} %copy-done, f32[8,3,512]{2,1,0:T(4,128)S(1)} %collective-permute-done.above.below, f32[8,3,512]{2,1,0:T(4,128)S(1)} %collective-permute-done.above.below), custom_call_target="tpu_custom_call" | custom-call | flops 524288000 | bytes 8388608 | tf_op jit(solution)/shard_map/pallas_call | solution.py:132
  17.2 0.2 collective-permute-start.1
  17.4 2.9 %shard_map.33 = (f32[8,4,64,128]{3,2,1,0:T(8,128)S(1)}, f32[64,512]{1,0:T(8,128)S(1)}, f32[64,512]{1,0:T(8,128)S(1)}) custom-call(s32[5]{0:T(128)S(1)} %stack.35.place, f32[8,256,512]{2,1,0:T(8,128)S(1)} %copy-done, f32[8,3,512]{2,1,0:T(4,128)S(1)} %collective-permute-done.above.below, f32[8,3,512]{2,1,0:T(4,128)S(1)} %collective-permute-done.above.below), custom_call_target="tpu_custom_call" | custom-call | flops 524288000 | bytes 8388608 | tf_op jit(solution)/shard_map/pallas_call | solution.py:132
  20.3 0.0 collective-permute-done.2
  20.3 0.0 collective-permute-done.3
  20.3 2.0 %collective-permute-done.1 = f32[64,512]{1,0:T(8,128)S(1)} collective-permute-done((f32[64,512]{1,0:T(8,128)S(1)}, f32[64,512]{1,0:T(8,128)S(1)}, u32[]{:S(2)}, u32[]{:S(2)}) %collective-permute-start.1) | collective-permute-done | bytes 131104 | tf_op jit(solution)/shard_map/ppermute | solution.py:288
  22.3 2.7 %collective-permute-start.4 = (f32[64,512]{1,0:T(8,128)S(1)}, f32[64,512]{1,0:T(8,128)S(1)}, u32[]{:S(2)}, u32[]{:S(2)}) collective-permute-start(f32[64,512]{1,0:T(8,128)S(1)} %add_add_fusion), channel_id=1, source_target_pairs={{0,8},{2,10},{4,12},{6,14},{8,0},{10,2},{12,4},{14,6},{1,9},{3,11}... | collective-permute-start | bytes 393224 | tf_op jit(solution)/shard_map/ppermute | solution.py:288
  25.0 1.3 %collective-permute-start.8 = (f32[1,256,512]{2,1,0:T(8,128)S(1)}, f32[1,256,512]{2,1,0:T(8,128)S(1)}, u32[]{:S(2)}, u32[]{:S(2)}) collective-permute-start(f32[1,256,512]{2,1,0:T(8,128)S(1)} %get-tuple-element.23), channel_id=1, source_target_pairs={{2,0},{4,2},{6,4},{8,6},{10,8},{12,10},{14,12},{3,1},{5,3},{7,5},{... | collective-permute-start | bytes 1572872 | tf_op jit(solution)/shard_map/ppermute | solution.py:384
  26.3 4.8 %collective-permute-done.4 = f32[64,512]{1,0:T(8,128)S(1)} collective-permute-done((f32[64,512]{1,0:T(8,128)S(1)}, f32[64,512]{1,0:T(8,128)S(1)}, u32[]{:S(2)}, u32[]{:S(2)}) %collective-permute-start.4) | collective-permute-done | bytes 131104 | tf_op jit(solution)/shard_map/ppermute | solution.py:288
  31.1 0.7 %collective-permute-start.5 = (f32[64,512]{1,0:T(8,128)S(1)}, f32[64,512]{1,0:T(8,128)S(1)}, u32[]{:S(2)}, u32[]{:S(2)}) collective-permute-start(f32[64,512]{1,0:T(8,128)S(1)} %add_multiply_fusion.rest_1_), channel_id=1, source_target_pairs={{0,2},{2,0},{4,6},{6,4},{8,10},{10,8},{12,14},{14,12},{1,3},{3,1},... | collective-permute-start | bytes 393224 | tf_op jit(solution)/shard_map/ppermute | solution.py:288
  31.8 0.0 collective-permute-start.6
  31.8 2.8 %collective-permute-start.7 = (f32[64,512]{1,0:T(8,128)S(1)}, f32[64,512]{1,0:T(8,128)S(1)}, u32[]{:S(2)}, u32[]{:S(2)}) collective-permute-start(f32[64,512]{1,0:T(8,128)S(1)} %add_multiply_fusion.rest_1_), channel_id=1, source_target_pairs={{0,6},{2,4},{4,2},{6,0},{8,14},{10,12},{12,10},{14,8},{1,7},{3,5},... | collective-permute-start | bytes 393224 | tf_op jit(solution)/shard_map/ppermute | solution.py:288
  34.7 2.6 %change.1.rest_7_ = f32[8,256,512]{2,1,0:T(8,128)} custom-call(s32[5]{0:T(128)S(1)} %stack.35.place, f32[8,4,64,128]{3,2,1,0:T(8,128)S(1)} %get-tuple-element.22.rest_0_, f32[8,4,64,128]{3,2,1,0:T(8,128)S(1)} %get-tuple-element.14.rest_0_.rest_1_, f32[8,4,64,128]{3,2,1,0:T(8,128)S(1)} %get-tuple-element.15.rest_1_.rest_2_, ...), custom_call_target="tpu_custom_call" | custom-call | flops 2097152000 | bytes 8388608 | tf_op jit(solution)/shard_map/change/pallas_call | solution.py:176
  37.3 1.6 %shard_map.34.rest_6_ = f32[8,256,512]{2,1,0:T(8,128)} custom-call(s32[5]{0:T(128)S(1)} %stack.35.place, f32[8,4,64,128]{3,2,1,0:T(8,128)S(1)} %get-tuple-element.22.rest_0_, f32[64,512]{1,0:T(8,128)S(1)} %add_multiply_fusion.rest_1_), custom_call_target="tpu_custom_call" | custom-call | flops 262144000 | bytes 2097152 | tf_op jit(solution)/shard_map/pallas_call | solution.py:272
  38.9 4.5 %collective-permute-done.8.first.final.rest_4_ = f32[1,256,512]{2,1,0:T(8,128)S(1)} collective-permute-done((f32[1,256,512]{2,1,0:T(8,128)S(1)}, f32[1,256,512]{2,1,0:T(8,128)S(1)}, u32[]{:S(2)}, u32[]{:S(2)}) %collective-permute-start.8) | collective-permute-done | bytes 524320 | tf_op jit(solution)/shard_map/ppermute | solution.py:384
  43.4 0.5 %rim.1 = f32[1,3,512]{2,1,0:T(4,128)S(1)} custom-call(s32[5]{0:T(128)S(1)} %stack.35.place, f32[1,256,512]{2,1,0:T(8,128)S(1)} %collective-permute-done.8.first.final.rest_4_, f32[1,256,512]{2,1,0:T(8,128)S(1)} %collective-permute-done.8.first.final.rest_4_), custom_call_target="tpu_custom_call" | custom-call | tf_op jit(solution)/shard_map/rim/pallas_call | solution.py:313
  44.0 0.1 collective-permute-start.9
  44.1 0.8 %collective-permute-done.5.rest_3_ = f32[64,512]{1,0:T(8,128)S(1)} collective-permute-done((f32[64,512]{1,0:T(8,128)S(1)}, f32[64,512]{1,0:T(8,128)S(1)}, u32[]{:S(2)}, u32[]{:S(2)}) %collective-permute-start.5) | collective-permute-done | bytes 131104 | tf_op jit(solution)/shard_map/ppermute | solution.py:288
  44.8 0.3 collective-permute-done.6.rest_4_
  45.1 0.0 collective-permute-done.7.rest_5_
  45.1 2.4 %shard_map.35 = f32[8,256,512]{2,1,0:T(8,128)} custom-call(s32[5]{0:T(128)S(1)} %stack.35.place, f32[8,4,64,128]{3,2,1,0:T(8,128)S(1)} %get-tuple-element.14.rest_0_.rest_1_, f32[8,4,64,128]{3,2,1,0:T(8,128)S(1)} %get-tuple-element.15.rest_1_.rest_2_, f32[8,4,64,128]{3,2,1,0:T(8,128)S(1)} %get-tuple-element.16.rest_2_.rest_3_, ...), custom_call_target="tpu_custom_call", output_to_operand_aliasing={{}: (7, {})} | custom-call | flops 786432000 | bytes 6291456 | tf_op jit(solution)/shard_map/pallas_call | solution.py:272
  47.6 0.0 collective-permute-done.9.rest_5_.rest_6_
  47.6 3.5 %last.1 = f32[8,256,512]{2,1,0:T(8,128)} custom-call(s32[5]{0:T(128)S(1)} %stack.35.place, f32[8,4,64,128]{3,2,1,0:T(8,128)S(1)} %get-tuple-element.22.rest_0_, f32[8,4,64,128]{3,2,1,0:T(8,128)S(1)} %get-tuple-element.14.rest_0_.rest_1_, f32[8,4,64,128]{3,2,1,0:T(8,128)S(1)} %get-tuple-element.15.rest_1_.rest_2_, ...), custom_call_target="tpu_custom_call", output_to_operand_aliasing={{}: (8, {})} | custom-call | flops 262144000 | bytes 1572864 | tf_op jit(solution)/shard_map/last/pallas_call | solution.py:230
  (2 shorter events, 0.1 us)
Async XLA Ops:
  0.7 3.4 %copy-start = (f32[8,256,512]{2,1,0:T(8,128)S(1)}, f32[8,256,512]{2,1,0:T(8,128)}, u32[]{:S(2)}) copy-start(f32[8,256,512]{2,1,0:T(8,128)} %image.9) | copy-start | bytes 12582916
  2.7 1.5 %collective-permute-start = (f32[8,3,512]{2,1,0:T(4,128)S(1)}, f32[8,3,512]{2,1,0:T(4,128)S(1)}, u32[]{:S(2)}, u32[]{:S(2)}) collective-permute-start(f32[8,3,512]{2,1,0:T(4,128)S(1)} %get-tuple-element.13), channel_id=1, source_target_pairs={{0,1},{1,0},{2,3},{3,2},{4,5},{5,4},{6,7},{7,6},{8,9},{9,8},{10,11... | collective-permute-start | bytes 147464 | tf_op jit(solution)/shard_map/ppermute | solution.py:380
  7.0 13.3 %collective-permute-start.2 = (f32[64,512]{1,0:T(8,128)S(1)}, f32[64,512]{1,0:T(8,128)S(1)}, u32[]{:S(2)}, u32[]{:S(2)}) collective-permute-start(f32[64,512]{1,0:T(8,128)S(1)} %get-tuple-element.19), channel_id=1, source_target_pairs={{0,4},{2,6},{4,0},{6,2},{8,12},{10,14},{12,8},{14,10},{1,5},{3,7},... | collective-permute-start | bytes 393224 | tf_op jit(solution)/shard_map/ppermute | solution.py:288
  12.9 7.4 %collective-permute-start.3 = (f32[64,512]{1,0:T(8,128)S(1)}, f32[64,512]{1,0:T(8,128)S(1)}, u32[]{:S(2)}, u32[]{:S(2)}) collective-permute-start(f32[64,512]{1,0:T(8,128)S(1)} %get-tuple-element.20), channel_id=1, source_target_pairs={{0,6},{2,4},{4,2},{6,0},{8,14},{10,12},{12,10},{14,8},{1,7},{3,5},... | collective-permute-start | bytes 393224 | tf_op jit(solution)/shard_map/ppermute | solution.py:288
  17.2 5.1 %collective-permute-start.1 = (f32[64,512]{1,0:T(8,128)S(1)}, f32[64,512]{1,0:T(8,128)S(1)}, u32[]{:S(2)}, u32[]{:S(2)}) collective-permute-start(f32[64,512]{1,0:T(8,128)S(1)} %get-tuple-element.18), channel_id=1, source_target_pairs={{0,2},{2,0},{4,6},{6,4},{8,10},{10,8},{12,14},{14,12},{1,3},{3,1},... | collective-permute-start | bytes 393224 | tf_op jit(solution)/shard_map/ppermute | solution.py:288
  22.3 8.8 %collective-permute-start.4 = (f32[64,512]{1,0:T(8,128)S(1)}, f32[64,512]{1,0:T(8,128)S(1)}, u32[]{:S(2)}, u32[]{:S(2)}) collective-permute-start(f32[64,512]{1,0:T(8,128)S(1)} %add_add_fusion), channel_id=1, source_target_pairs={{0,8},{2,10},{4,12},{6,14},{8,0},{10,2},{12,4},{14,6},{1,9},{3,11}... | collective-permute-start | bytes 393224 | tf_op jit(solution)/shard_map/ppermute | solution.py:288
  25.0 18.5 %collective-permute-start.8 = (f32[1,256,512]{2,1,0:T(8,128)S(1)}, f32[1,256,512]{2,1,0:T(8,128)S(1)}, u32[]{:S(2)}, u32[]{:S(2)}) collective-permute-start(f32[1,256,512]{2,1,0:T(8,128)S(1)} %get-tuple-element.23), channel_id=1, source_target_pairs={{2,0},{4,2},{6,4},{8,6},{10,8},{12,10},{14,12},{3,1},{5,3},{7,5},{... | collective-permute-start | bytes 1572872 | tf_op jit(solution)/shard_map/ppermute | solution.py:384
  31.1 13.7 %collective-permute-start.5 = (f32[64,512]{1,0:T(8,128)S(1)}, f32[64,512]{1,0:T(8,128)S(1)}, u32[]{:S(2)}, u32[]{:S(2)}) collective-permute-start(f32[64,512]{1,0:T(8,128)S(1)} %add_multiply_fusion.rest_1_), channel_id=1, source_target_pairs={{0,2},{2,0},{4,6},{6,4},{8,10},{10,8},{12,14},{14,12},{1,3},{3,1},... | collective-permute-start | bytes 393224 | tf_op jit(solution)/shard_map/ppermute | solution.py:288
  31.8 13.3 %collective-permute-start.6 = (f32[64,512]{1,0:T(8,128)S(1)}, f32[64,512]{1,0:T(8,128)S(1)}, u32[]{:S(2)}, u32[]{:S(2)}) collective-permute-start(f32[64,512]{1,0:T(8,128)S(1)} %add_multiply_fusion.rest_1_), channel_id=1, source_target_pairs={{0,4},{2,6},{4,0},{6,2},{8,12},{10,14},{12,8},{14,10},{1,5},{3,7},... | collective-permute-start | bytes 393224 | tf_op jit(solution)/shard_map/ppermute | solution.py:288
  31.8 13.3 %collective-permute-start.7 = (f32[64,512]{1,0:T(8,128)S(1)}, f32[64,512]{1,0:T(8,128)S(1)}, u32[]{:S(2)}, u32[]{:S(2)}) collective-permute-start(f32[64,512]{1,0:T(8,128)S(1)} %add_multiply_fusion.rest_1_), channel_id=1, source_target_pairs={{0,6},{2,4},{4,2},{6,0},{8,14},{10,12},{12,10},{14,8},{1,7},{3,5},... | collective-permute-start | bytes 393224 | tf_op jit(solution)/shard_map/ppermute | solution.py:288
  44.0 3.6 %collective-permute-start.9 = (f32[1,3,512]{2,1,0:T(4,128)S(1)}, f32[1,3,512]{2,1,0:T(4,128)S(1)}, u32[]{:S(2)}, u32[]{:S(2)}) collective-permute-start(f32[1,3,512]{2,1,0:T(4,128)S(1)} %rim.1), channel_id=1, source_target_pairs={{0,1},{1,0},{2,3},{3,2},{4,5},{5,4},{6,7},{7,6},{8,9},{9,8},{10,11... | collective-permute-start | bytes 18440 | tf_op jit(solution)/shard_map/ppermute | solution.py:411

commit v4 on v3

--- a/solution.py
+++ b/solution.py
@@ -51,6 +51,21 @@
     far_left = lane_shift(left, -2)
     far_right = lane_shift(right, 2)
     return [(far_left[j] + left[j]) + (after[j] + far_right[j]) for j in range(tiles_n)]
+
+
+def located(kernel, parts_n, rows_n):
+    def run(*refs):
+        date, row = lax.axis_index("date"), lax.axis_index("row")
+        place = [
+            date & (parts_n - 1),
+            row * rows_n,
+            (row > 0).astype(jnp.int32),
+            (row < lax.axis_size("row") - 1).astype(jnp.int32),
+            (date == lax.axis_size("date") - 1).astype(jnp.int32),
+        ]
+        return kernel(place, *refs)
+
+    return run
 
 
 def part_row(place, k, part_rows):
@@ -118,29 +133,28 @@
             held[t, j, end : end + RADIUS, :] = below[t, :, pl.ds(j * LANES, LANES)] * keep
 
 
-SCALARS = pl.BlockSpec(memory_space=pltpu.SMEM)
 WHOLE = pl.BlockSpec(memory_space=pltpu.VMEM)
 OUTER = pl.BlockSpec(memory_space=pltpu.HBM)
 
 
-def window_call(image, above, below, place, k, parts_n, rows_total, dates_total):
+def window_call(image, above, below, k, parts_n, rows_total, dates_total):
     dates_n, rows_n, cols_n = image.shape
     tiles_n = cols_n // LANES
     part_rows = rows_n // parts_n
     outs = 2 if k == 0 else 1
     f32 = jnp.float32
     return pl.pallas_call(
-        functools.partial(window_kernel, k, rows_total, float(dates_total)),
+        located(functools.partial(window_kernel, k, rows_total, float(dates_total)), parts_n, rows_n),
         out_shape=[
             jax.ShapeDtypeStruct((dates_n, tiles_n, part_rows, LANES), f32),
         ]
         + [jax.ShapeDtypeStruct((part_rows, cols_n), f32)] * outs,
-        in_specs=[SCALARS, WHOLE, WHOLE, WHOLE],
+        in_specs=[WHOLE, WHOLE, WHOLE],
         out_specs=[WHOLE] * (1 + outs),
         scratch_shapes=[pltpu.VMEM((dates_n, tiles_n, part_rows + 2 * SUBLANES, LANES), f32)],
         compiler_params=pltpu.CompilerParams(vmem_limit_bytes=12 * MIB),
         cost_estimate=pl.CostEstimate(flops=500 * image.size, bytes_accessed=8 * image.size, transcendentals=0),
-    )(place, image, above, below)
+    )(image, above, below)
 
 
 def change_kernel(parts_n, place, *rest):
@@ -168,15 +182,15 @@
         copy.wait()
 
 
-def change_call(sums, place):
+def change_call(sums):
     parts_n = len(sums)
     dates_n, tiles_n, part_rows, _ = sums[0].shape
     cols_n = tiles_n * LANES
     size = parts_n * sums[0].size
     return pl.pallas_call(
-        functools.partial(change_kernel, parts_n),
+        located(functools.partial(change_kernel, parts_n), parts_n, parts_n * part_rows),
         out_shape=jax.ShapeDtypeStruct((dates_n, parts_n * part_rows, cols_n), jnp.float32),
-        in_specs=[SCALARS] + [WHOLE] * parts_n,
+        in_specs=[WHOLE] * parts_n,
         out_specs=OUTER,
         scratch_shapes=[
             pltpu.VMEM((parts_n, dates_n - 1, part_rows, cols_n), jnp.float32),
@@ -185,7 +199,7 @@
         compiler_params=pltpu.CompilerParams(vmem_limit_bytes=12 * MIB),
         cost_estimate=pl.CostEstimate(flops=2000 * size, bytes_accessed=8 * size, transcendentals=size),
         name="change",
-    )(place, *sums)
+    )(*sums)
 
 
 def last_kernel(parts_n, unroll, place, *rest):
@@ -221,16 +235,16 @@
     copy.wait()
 
 
-def last_call(sums, pieces, above, below, place, change):
+def last_call(sums, pieces, above, below, change):
     parts_n = len(sums)
     _, tiles_n, part_rows, _ = sums[0].shape
     rows_n, cols_n = parts_n * part_rows, tiles_n * LANES
-    inputs = parts_n + len(pieces) + 3
+    inputs = parts_n + len(pieces) + 2
     unroll = 8 if part_rows % (8 * SUBLANES) == 0 else 1
     return pl.pallas_call(
-        functools.partial(last_kernel, parts_n, unroll),
+        located(functools.partial(last_kernel, parts_n, unroll), parts_n, rows_n),
         out_shape=jax.ShapeDtypeStruct(change.shape, jnp.float32),
-        in_specs=[SCALARS] + [WHOLE] * (inputs - 1) + [OUTER],
+        in_specs=[WHOLE] * inputs + [OUTER],
         out_specs=OUTER,
         scratch_shapes=[
             pltpu.VMEM((1, tiles_n, rows_n + 2 * SUBLANES, LANES), jnp.float32),
@@ -241,7 +255,7 @@
         compiler_params=pltpu.CompilerParams(vmem_limit_bytes=12 * MIB),
         cost_estimate=pl.CostEstimate(flops=2000 * rows_n * cols_n, bytes_accessed=12 * rows_n * cols_n, transcendentals=0),
         name="last",
-    )(place, *sums, *pieces, above, below, change)
+    )(*sums, *pieces, above, below, change)
 
 
 def scale_kernel(ks, place, *rest):
@@ -263,25 +277,25 @@
         copy.wait()
 
 
-def scale_call(sums, scales, place, ks, rows_n, filtered):
+def scale_call(sums, scales, ks, rows_n, filtered):
     n = len(ks)
     dates_n, tiles_n, part_rows, _ = sums[0].shape
     cols_n = tiles_n * LANES
     size = n * sums[0].size
     aliased = [] if filtered is None else [filtered]
     return pl.pallas_call(
-        functools.partial(scale_kernel, ks),
-        in_specs=[SCALARS] + [WHOLE] * (2 * n) + [OUTER] * len(aliased),
+        located(functools.partial(scale_kernel, ks), rows_n // part_rows, rows_n),
+        in_specs=[WHOLE] * (2 * n) + [OUTER] * len(aliased),
         out_specs=OUTER,
         out_shape=jax.ShapeDtypeStruct((dates_n, rows_n, cols_n), jnp.float32),
         scratch_shapes=[
             pltpu.VMEM((n, dates_n, part_rows, cols_n), jnp.float32),
             pltpu.SemaphoreType.DMA((n, dates_n)),
         ],
-        input_output_aliases={2 * n + 1: 0} if aliased else {},
+        input_output_aliases={2 * n: 0} if aliased else {},
         compiler_params=pltpu.CompilerParams(vmem_limit_bytes=12 * MIB),
         cost_estimate=pl.CostEstimate(flops=1000 * size, bytes_accessed=8 * size, transcendentals=0),
-    )(place, *sums, *scales, *aliased)
+    )(*sums, *scales, *aliased)
 
 
 def crossed(block, axis, bits):
@@ -308,45 +322,57 @@
     rim[...] = jnp.where(is_first, tail[:, SUBLANES - RADIUS :, :], head[:, :RADIUS, :])
 
 
-def rim_call(pieces, place):
+def rim_call(pieces):
     first, final = pieces[0], pieces[-1]
     return pl.pallas_call(
-        rim_kernel,
+        located(rim_kernel, 1, final.shape[1]),
         out_shape=jax.ShapeDtypeStruct((first.shape[0], RADIUS, first.shape[2]), jnp.float32),
-        in_specs=[SCALARS, WHOLE, WHOLE],
+        in_specs=[WHOLE, WHOLE],
         out_specs=WHOLE,
         compiler_params=pltpu.CompilerParams(vmem_limit_bytes=4 * MIB),
         name="rim",
-    )(place, first, final)
-
-
-def prepare_kernel(place, image, rim, early, held, sem):
+    )(first, final)
+
+
+def prepare_kernel(place, image, rim, *rest):
+    pieces, (held, sem) = rest[:-2], rest[-2:]
     rows_n = image.shape[1]
     is_first = place[2] == 0
     start = pl.multiple_of(jnp.where(is_first, rows_n - SUBLANES, 0), SUBLANES)
     edge = pltpu.make_async_copy(image.at[:, pl.ds(start, SUBLANES), :], held, sem.at[0])
     edge.start()
-    copy = pltpu.make_async_copy(image.at[pl.ds(0, 1), pl.ds(0, early.shape[1]), :], early, sem.at[1])
-    copy.start()
+    copies, row = [], 0
+    for i, piece in enumerate(pieces):
+        copy = pltpu.make_async_copy(image.at[pl.ds(0, 1), pl.ds(row, piece.shape[1]), :], piece, sem.at[i + 1])
+        copy.start()
+        copies.append(copy)
+        row += piece.shape[1]
     edge.wait()
     rim[...] = jnp.where(is_first, held[:, SUBLANES - RADIUS :, :], held[:, :RADIUS, :])
-    copy.wait()
-
-
-def prepare_call(image, place, cut):
-    dates_n, _, cols_n = image.shape
-    return pl.pallas_call(
-        prepare_kernel,
-        out_shape=[
-            jax.ShapeDtypeStruct((dates_n, RADIUS, cols_n), jnp.float32),
-            jax.ShapeDtypeStruct((1, cut, cols_n), jnp.float32),
+    for copy in copies:
+        copy.wait()
+
+
+def prepare_call(image, cuts):
+    dates_n, rows_n, cols_n = image.shape
+    return pl.pallas_call(
+        located(prepare_kernel, 1, rows_n),
+        out_shape=[jax.ShapeDtypeStruct((dates_n, RADIUS, cols_n), jnp.float32)]
+        + [jax.ShapeDtypeStruct((1, cut, cols_n), jnp.float32) for cut in cuts],
+        in_specs=[OUTER],
+        out_specs=[WHOLE] * (1 + len(cuts)),
+        scratch_shapes=[
+            pltpu.VMEM((dates_n, SUBLANES, cols_n), jnp.float32),
+            pltpu.SemaphoreType.DMA((1 + len(cuts),)),
         ],
-        in_specs=[SCALARS, OUTER],
-        out_specs=[WHOLE, WHOLE],
-        scratch_shapes=[pltpu.VMEM((dates_n, SUBLANES, cols_n), jnp.float32), pltpu.SemaphoreType.DMA((2,))],
         compiler_params=pltpu.CompilerParams(vmem_limit_bytes=4 * MIB),
         name="prepare",
-    )(place, pltpu.with_memory_space_constraint(image, pltpu.HBM))
+    )(pltpu.with_memory_space_constraint(image, pltpu.HBM))
+
+
+def early_rows(rows_n):
+    cut = rows_n * 11 // 16 // SUBLANES * SUBLANES
+    return cut if cut >= SUBLANES else rows_n
 
 
 def parts_of(group, rows_n):
@@ -359,34 +385,26 @@
 def on_device(image):
     dates_n, rows_n, _ = image.shape
     row_groups, date_groups = lax.axis_size("row"), lax.axis_size("date")
-    row_index, date_index = lax.axis_index("row"), lax.axis_index("date")
+    row_index = lax.axis_index("row")
     rows_total = rows_n * row_groups
     dates_total = dates_n * date_groups
     parts_n = parts_of(date_groups, rows_n)
 
-    place = jnp.stack(
-        [
-            date_index & (parts_n - 1),
-            row_index * rows_n,
-            (row_index > 0).astype(jnp.int32),
-            (row_index < row_groups - 1).astype(jnp.int32),
-            (date_index == date_groups - 1).astype(jnp.int32),
-        ]
-    ).astype(jnp.int32)
-    cut = rows_n
+    cut = early_rows(rows_n)
+    cuts = [cut, rows_n - cut] if cut < rows_n else [cut]
     route = [(i + 1, i) for i in range(date_groups - 1)]
     if row_groups == 2:
-        rim, early = prepare_call(image, place, cut)
+        rim, *pieces = prepare_call(image, cuts)
         above = below = lax.ppermute(rim, "row", [(0, 1), (1, 0)])
     else:
-        early = image[:1, :cut]
-        above, below = halo_rows([image], "row", place[2] == 0)
-    after = [lax.ppermute(early, "date", route)]
-    if cut < rows_n:
-        after.append(lax.ppermute(image[:1, cut:], "date", route))
+        pieces = [image[:1, :cut], image[:1, cut:]][: len(cuts)]
+        above, below = halo_rows([image], "row", row_index == 0)
+    after = [lax.ppermute(pieces[0], "date", route)]
+    if len(pieces) > 1:
+        after.append(lax.ppermute(pieces[1], "date", route))
     sums, parts = [], []
     for k in range(parts_n):
-        made = window_call(image, above, below, place, k, parts_n, rows_total, dates_total)
+        made = window_call(image, above, below, k, parts_n, rows_total, dates_total)
         sums.append(made[0])
         parts.append(made[1])
         if k == 0:
@@ -406,15 +424,15 @@
     for k in range(1, parts_n):
         scales.append(crossed(scales[0], "date", k))
 
-    change = change_call(sums, place)
+    change = change_call(sums)
     if row_groups == 2:
-        after_above = after_below = lax.ppermute(rim_call(after, place), "row", [(0, 1), (1, 0)])
+        after_above = after_below = lax.ppermute(rim_call(after), "row", [(0, 1), (1, 0)])
     else:
-        after_above, after_below = halo_rows(after, "row", place[2] == 0)
-    change = last_call(sums, after, after_above, after_below, place, change)
-    filtered = scale_call(sums[:1], scales[:1], place, (0,), rows_n, None)
+        after_above, after_below = halo_rows(after, "row", row_index == 0)
+    change = last_call(sums, after, after_above, after_below, change)
+    filtered = scale_call(sums[:1], scales[:1], (0,), rows_n, None)
     if parts_n > 1:
-        filtered = scale_call(sums[1:], scales[1:], place, tuple(range(1, parts_n)), rows_n, filtered)
+        filtered = scale_call(sums[1:], scales[1:], tuple(range(1, parts_n)), rows_n, filtered)
     return filtered, change
 
 

time: 51.5 us -> 48.3 us (0.938)
  Pallas kernels: 24.1 us -> 18.5 us
  waiting for transfers between devices: 13.3 us -> 14.7 us
  starting transfers between devices: 12.8 us -> 14 us
    pallas_call x10, Pallas kernels: 24.1 us -> 18.5 us  [the longest x4 9.27 us: window_call(): pl.pallas_call(located(functools.partial(window_kernel, k, rows_total, fl...]
    ppermute x2 -> x3, waiting for transfers between devices: 4.53 us -> 6.77 us  [the longest x1 6.66 us: on_device(): after.append(lax.ppermute(pieces[1], 'date', route))]
    ppermute x2 -> x3, starting transfers between devices: 1.35 us -> 2.64 us  [the longest x1 1.29 us: on_device(): after.append(lax.ppermute(pieces[1], 'date', route))]
    ppermute x7, waiting for transfers between devices: 7.9 us -> 7.01 us  [crossed(): lax.ppermute(block, axis, [(i, i ^ bits) for i in range(lax.axis_size(axi...]
  transfers between devices with their start and end apart: 10 -> 11, of which waited for: 6 -> 5; matrix products, arithmetic and copies ran while one was open for 0% -> 0% of each run, Pallas kernels for 31% -> 27%
where the time goes in v4:
time: 48.3 us; the launch traced here: 48.1 us
  Pallas kernels  18.5 us (38%)
  waiting for transfers between devices  14.7 us (30%)
  starting transfers between devices  14 us (29%)
  between operations  0.79 us (2%)
    ppermute x7, starting transfers between devices, crossed(): lax.ppermute(block, axis, [(i, i ^ bits) for i in range(lax.axis_size(axi...  10.8 us
    pallas_call x4, Pallas kernels, window_call(): pl.pallas_call(located(functools.partial(window_kernel, k, rows_total, fl...  9.27 us
    ppermute x7, waiting for transfers between devices, crossed(): lax.ppermute(block, axis, [(i, i ^ bits) for i in range(lax.axis_size(axi...  7.01 us
    ppermute x1, waiting for transfers between devices, on_device(): after.append(lax.ppermute(pieces[1], 'date', route))  6.66 us
    pallas_call x1, Pallas kernels, last_call(): pl.pallas_call(located(functools.partial(last_kernel, parts_n, unroll), p...  3 us
    pallas_call x2, Pallas kernels, scale_call(): pl.pallas_call(located(functools.partial(scale_kernel, ks), rows_n // par...  2.91 us
    pallas_call x1, Pallas kernels, change_call(): pl.pallas_call(located(functools.partial(change_kernel, parts_n), parts_n...  2.07 us
    ppermute x1, starting transfers between devices, on_device(): after.append(lax.ppermute(pieces[1], 'date', route))  1.29 us
  transfers between devices with their start and end apart: 11, of which 5 were waited for; matrix products, arithmetic and copies ran while one was open for 0% of the time, Pallas kernels for 27%

profile of v4, /device:TPU:0, one launch (start us, length us, event | category | flops | bytes accessed | tf_op | source)
XLA Modules:
  0.0 48.1 jit_solution(10472544131104337312)
XLA Ops:
  0.6 0.0 copy-start
  0.6 1.3 %prepare.1 = (f32[8,3,512]{2,1,0:T(4,128)S(1)}, f32[1,176,512]{2,1,0:T(8,128)S(1)}, f32[1,80,512]{2,1,0:T(8,128)S(1)}) custom-call(f32[8,256,512]{2,1,0:T(8,128)} %refs_0_.9), custom_call_target="tpu_custom_call" | custom-call | tf_op jit(solution)/shard_map/prepare/pallas_call | solution.py:358
  1.9 0.6 %collective-permute-start = (f32[8,3,512]{2,1,0:T(4,128)S(1)}, f32[8,3,512]{2,1,0:T(4,128)S(1)}, u32[]{:S(2)}, u32[]{:S(2)}) collective-permute-start(f32[8,3,512]{2,1,0:T(4,128)S(1)} %get-tuple-element.14), channel_id=1, source_target_pairs={{0,1},{1,0},{2,3},{3,2},{4,5},{5,4},{6,7},{7,6},{8,9},{9,8},{10,11... | collective-permute-start | bytes 147464 | tf_op jit(solution)/shard_map/ppermute | solution.py:398
  2.5 0.9 %collective-permute-done.refs_1_.refs_2_ = f32[8,3,512]{2,1,0:T(4,128)S(1)} collective-permute-done((f32[8,3,512]{2,1,0:T(4,128)S(1)}, f32[8,3,512]{2,1,0:T(4,128)S(1)}, u32[]{:S(2)}, u32[]{:S(2)}) %collective-permute-start) | collective-permute-done | bytes 49184 | tf_op jit(solution)/shard_map/ppermute | solution.py:398
  3.4 0.0 copy-done
  3.4 2.3 %shard_map.30 = (f32[8,4,64,128]{3,2,1,0:T(8,128)S(1)}, f32[64,512]{1,0:T(8,128)S(1)}) custom-call(f32[8,256,512]{2,1,0:T(8,128)S(1)} %copy-done, f32[8,3,512]{2,1,0:T(4,128)S(1)} %collective-permute-done.refs_1_.refs_2_, f32[8,3,512]{2,1,0:T(4,128)S(1)} %collective-permute-done.refs_1_.refs_2_), custom_call_target="tpu_custom_call" | custom-call | flops 524288000 | bytes 8388608 | tf_op jit(solution)/shard_map/pallas_call | solution.py:146
  5.7 2.9 %collective-permute-start.1 = (f32[64,512]{1,0:T(8,128)S(1)}, f32[64,512]{1,0:T(8,128)S(1)}, u32[]{:S(2)}, u32[]{:S(2)}) collective-permute-start(f32[64,512]{1,0:T(8,128)S(1)} %get-tuple-element.19), channel_id=1, source_target_pairs={{0,2},{2,0},{4,6},{6,4},{8,10},{10,8},{12,14},{14,12},{1,3},{3,1},... | collective-permute-start | bytes 393224 | tf_op jit(solution)/shard_map/ppermute | solution.py:302
  8.6 2.3 %shard_map.31 = (f32[8,4,64,128]{3,2,1,0:T(8,128)S(1)}, f32[64,512]{1,0:T(8,128)S(1)}) custom-call(f32[8,256,512]{2,1,0:T(8,128)S(1)} %copy-done, f32[8,3,512]{2,1,0:T(4,128)S(1)} %collective-permute-done.refs_1_.refs_2_, f32[8,3,512]{2,1,0:T(4,128)S(1)} %collective-permute-done.refs_1_.refs_2_), custom_call_target="tpu_custom_call" | custom-call | flops 524288000 | bytes 8388608 | tf_op jit(solution)/shard_map/pallas_call | solution.py:146
  10.9 1.6 %collective-permute-start.2 = (f32[64,512]{1,0:T(8,128)S(1)}, f32[64,512]{1,0:T(8,128)S(1)}, u32[]{:S(2)}, u32[]{:S(2)}) collective-permute-start(f32[64,512]{1,0:T(8,128)S(1)} %get-tuple-element.20), channel_id=1, source_target_pairs={{0,4},{2,6},{4,0},{6,2},{8,12},{10,14},{12,8},{14,10},{1,5},{3,7},... | collective-permute-start | bytes 393224 | tf_op jit(solution)/shard_map/ppermute | solution.py:302
  12.6 2.3 %shard_map.32 = (f32[8,4,64,128]{3,2,1,0:T(8,128)S(1)}, f32[64,512]{1,0:T(8,128)S(1)}) custom-call(f32[8,256,512]{2,1,0:T(8,128)S(1)} %copy-done, f32[8,3,512]{2,1,0:T(4,128)S(1)} %collective-permute-done.refs_1_.refs_2_, f32[8,3,512]{2,1,0:T(4,128)S(1)} %collective-permute-done.refs_1_.refs_2_), custom_call_target="tpu_custom_call" | custom-call | flops 524288000 | bytes 8388608 | tf_op jit(solution)/shard_map/pallas_call | solution.py:146
  14.9 0.1 collective-permute-start.3
  15.0 2.3 %shard_map.33 = (f32[8,4,64,128]{3,2,1,0:T(8,128)S(1)}, f32[64,512]{1,0:T(8,128)S(1)}, f32[64,512]{1,0:T(8,128)S(1)}) custom-call(f32[8,256,512]{2,1,0:T(8,128)S(1)} %copy-done, f32[8,3,512]{2,1,0:T(4,128)S(1)} %collective-permute-done.refs_1_.refs_2_, f32[8,3,512]{2,1,0:T(4,128)S(1)} %collective-permute-done.refs_1_.refs_2_), custom_call_target="tpu_custom_call" | custom-call | flops 524288000 | bytes 8388608 | tf_op jit(solution)/shard_map/pallas_call | solution.py:146
  17.3 0.0 collective-permute-done.1
  17.3 0.0 collective-permute-done.2
  17.4 3.5 %collective-permute-done.3 = f32[64,512]{1,0:T(8,128)S(1)} collective-permute-done((f32[64,512]{1,0:T(8,128)S(1)}, f32[64,512]{1,0:T(8,128)S(1)}, u32[]{:S(2)}, u32[]{:S(2)}) %collective-permute-start.3) | collective-permute-done | bytes 131104 | tf_op jit(solution)/shard_map/ppermute | solution.py:302
  20.9 2.7 %collective-permute-start.4 = (f32[64,512]{1,0:T(8,128)S(1)}, f32[64,512]{1,0:T(8,128)S(1)}, u32[]{:S(2)}, u32[]{:S(2)}) collective-permute-start(f32[64,512]{1,0:T(8,128)S(1)} %add_add_fusion), channel_id=1, source_target_pairs={{0,8},{2,10},{4,12},{6,14},{8,0},{10,2},{12,4},{14,6},{1,9},{3,11}... | collective-permute-start | bytes 393224 | tf_op jit(solution)/shard_map/ppermute | solution.py:302
  23.6 1.3 %collective-permute-start.8 = (f32[1,176,512]{2,1,0:T(8,128)S(1)}, f32[1,176,512]{2,1,0:T(8,128)S(1)}, u32[]{:S(2)}, u32[]{:S(2)}) collective-permute-start(f32[1,176,512]{2,1,0:T(8,128)S(1)} %get-tuple-element.24), channel_id=1, source_target_pairs={{2,0},{4,2},{6,4},{8,6},{10,8},{12,10},{14,12},{3,1},{5,3},{7,5},{... | collective-permute-start | bytes 1081352 | tf_op jit(solution)/shard_map/ppermute | solution.py:402
  24.9 1.3 %collective-permute-start.9 = (f32[1,80,512]{2,1,0:T(8,128)S(1)}, f32[1,80,512]{2,1,0:T(8,128)S(1)}, u32[]{:S(2)}, u32[]{:S(2)}) collective-permute-start(f32[1,80,512]{2,1,0:T(8,128)S(1)} %get-tuple-element.25), channel_id=1, source_target_pairs={{2,0},{4,2},{6,4},{8,6},{10,8},{12,10},{14,12},{3,1},{5,3},{7,5},{... | collective-permute-start | bytes 491528 | tf_op jit(solution)/shard_map/ppermute | solution.py:404
  26.2 3.5 %collective-permute-done.4 = f32[64,512]{1,0:T(8,128)S(1)} collective-permute-done((f32[64,512]{1,0:T(8,128)S(1)}, f32[64,512]{1,0:T(8,128)S(1)}, u32[]{:S(2)}, u32[]{:S(2)}) %collective-permute-start.4) | collective-permute-done | bytes 131104 | tf_op jit(solution)/shard_map/ppermute | solution.py:302
  29.7 0.1 collective-permute-start.5
  29.7 1.8 %collective-permute-start.6 = (f32[64,512]{1,0:T(8,128)S(1)}, f32[64,512]{1,0:T(8,128)S(1)}, u32[]{:S(2)}, u32[]{:S(2)}) collective-permute-start(f32[64,512]{1,0:T(8,128)S(1)} %add_multiply_fusion.refs_1_), channel_id=1, source_target_pairs={{0,4},{2,6},{4,0},{6,2},{8,12},{10,14},{12,8},{14,10},{1,5},{3,7},... | collective-permute-start | bytes 393224 | tf_op jit(solution)/shard_map/ppermute | solution.py:302
  31.5 1.7 %collective-permute-start.7 = (f32[64,512]{1,0:T(8,128)S(1)}, f32[64,512]{1,0:T(8,128)S(1)}, u32[]{:S(2)}, u32[]{:S(2)}) collective-permute-start(f32[64,512]{1,0:T(8,128)S(1)} %add_multiply_fusion.refs_1_), channel_id=1, source_target_pairs={{0,6},{2,4},{4,2},{6,0},{8,14},{10,12},{12,10},{14,8},{1,7},{3,5},... | collective-permute-start | bytes 393224 | tf_op jit(solution)/shard_map/ppermute | solution.py:302
  33.2 2.1 %change.1.refs_8_ = f32[8,256,512]{2,1,0:T(8,128)} custom-call(f32[8,4,64,128]{3,2,1,0:T(8,128)S(1)} %get-tuple-element.23.refs_0_, f32[8,4,64,128]{3,2,1,0:T(8,128)S(1)} %get-tuple-element.15.refs_0_.refs_1_, f32[8,4,64,128]{3,2,1,0:T(8,128)S(1)} %get-tuple-element.16.refs_1_.refs_2_, f32[8,4,64,128]{3,2,1,0:T(8,128)S(1)} %get-tuple-element.17.refs_2_.refs_3_), custom_call_target="tpu_custom_call" | custom-call | flops 2097152000 | bytes 8388608 | tf_op jit(solution)/shard_map/change/pallas_call | solution.py:190
  35.3 6.7 %collective-permute-done.9.refs_1_.refs_5_ = f32[1,80,512]{2,1,0:T(8,128)S(1)} collective-permute-done((f32[1,80,512]{2,1,0:T(8,128)S(1)}, f32[1,80,512]{2,1,0:T(8,128)S(1)}, u32[]{:S(2)}, u32[]{:S(2)}) %collective-permute-start.9) | collective-permute-done | bytes 163872 | tf_op jit(solution)/shard_map/ppermute | solution.py:404
  42.0 0.0 collective-permute-done.8.refs_0_.refs_4_
  42.0 0.1 collective-permute-start.10
  42.1 1.0 %shard_map.34.refs_6_ = f32[8,256,512]{2,1,0:T(8,128)} custom-call(f32[8,4,64,128]{3,2,1,0:T(8,128)S(1)} %get-tuple-element.23.refs_0_, f32[64,512]{1,0:T(8,128)S(1)} %add_multiply_fusion.refs_1_), custom_call_target="tpu_custom_call" | custom-call | flops 262144000 | bytes 2097152 | tf_op jit(solution)/shard_map/pallas_call | solution.py:286
  43.1 0.1 collective-permute-done.10.refs_6_.refs_7_
  43.2 3.0 %last.1 = f32[8,256,512]{2,1,0:T(8,128)} custom-call(f32[8,4,64,128]{3,2,1,0:T(8,128)S(1)} %get-tuple-element.23.refs_0_, f32[8,4,64,128]{3,2,1,0:T(8,128)S(1)} %get-tuple-element.15.refs_0_.refs_1_, f32[8,4,64,128]{3,2,1,0:T(8,128)S(1)} %get-tuple-element.16.refs_1_.refs_2_, ...), custom_call_target="tpu_custom_call", output_to_operand_aliasing={{}: (8, {})} | custom-call | flops 262144000 | bytes 1572864 | tf_op jit(solution)/shard_map/last/pallas_call | solution.py:244
  46.2 0.0 collective-permute-done.5.refs_3_
  46.2 0.0 collective-permute-done.6.refs_4_
  46.2 0.0 collective-permute-done.7.refs_5_
  46.3 1.9 %shard_map.35 = f32[8,256,512]{2,1,0:T(8,128)} custom-call(f32[8,4,64,128]{3,2,1,0:T(8,128)S(1)} %get-tuple-element.15.refs_0_.refs_1_, f32[8,4,64,128]{3,2,1,0:T(8,128)S(1)} %get-tuple-element.16.refs_1_.refs_2_, f32[8,4,64,128]{3,2,1,0:T(8,128)S(1)} %get-tuple-element.17.refs_2_.refs_3_, ...), custom_call_target="tpu_custom_call", output_to_operand_aliasing={{}: (6, {})} | custom-call | flops 786432000 | bytes 6291456 | tf_op jit(solution)/shard_map/pallas_call | solution.py:286
  (3 shorter events, 0.1 us)
Async XLA Ops:
  0.6 2.8 %copy-start = (f32[8,256,512]{2,1,0:T(8,128)S(1)}, f32[8,256,512]{2,1,0:T(8,128)}, u32[]{:S(2)}) copy-start(f32[8,256,512]{2,1,0:T(8,128)} %refs_0_.9) | copy-start | bytes 12582916
  1.9 1.5 %collective-permute-start = (f32[8,3,512]{2,1,0:T(4,128)S(1)}, f32[8,3,512]{2,1,0:T(4,128)S(1)}, u32[]{:S(2)}, u32[]{:S(2)}) collective-permute-start(f32[8,3,512]{2,1,0:T(4,128)S(1)} %get-tuple-element.14), channel_id=1, source_target_pairs={{0,1},{1,0},{2,3},{3,2},{4,5},{5,4},{6,7},{7,6},{8,9},{9,8},{10,11... | collective-permute-start | bytes 147464 | tf_op jit(solution)/shard_map/ppermute | solution.py:398
  5.7 11.6 %collective-permute-start.1 = (f32[64,512]{1,0:T(8,128)S(1)}, f32[64,512]{1,0:T(8,128)S(1)}, u32[]{:S(2)}, u32[]{:S(2)}) collective-permute-start(f32[64,512]{1,0:T(8,128)S(1)} %get-tuple-element.19), channel_id=1, source_target_pairs={{0,2},{2,0},{4,6},{6,4},{8,10},{10,8},{12,14},{14,12},{1,3},{3,1},... | collective-permute-start | bytes 393224 | tf_op jit(solution)/shard_map/ppermute | solution.py:302
  10.9 6.4 %collective-permute-start.2 = (f32[64,512]{1,0:T(8,128)S(1)}, f32[64,512]{1,0:T(8,128)S(1)}, u32[]{:S(2)}, u32[]{:S(2)}) collective-permute-start(f32[64,512]{1,0:T(8,128)S(1)} %get-tuple-element.20), channel_id=1, source_target_pairs={{0,4},{2,6},{4,0},{6,2},{8,12},{10,14},{12,8},{14,10},{1,5},{3,7},... | collective-permute-start | bytes 393224 | tf_op jit(solution)/shard_map/ppermute | solution.py:302
  14.9 6.0 %collective-permute-start.3 = (f32[64,512]{1,0:T(8,128)S(1)}, f32[64,512]{1,0:T(8,128)S(1)}, u32[]{:S(2)}, u32[]{:S(2)}) collective-permute-start(f32[64,512]{1,0:T(8,128)S(1)} %get-tuple-element.21), channel_id=1, source_target_pairs={{0,6},{2,4},{4,2},{6,0},{8,14},{10,12},{12,10},{14,8},{1,7},{3,5},... | collective-permute-start | bytes 393224 | tf_op jit(solution)/shard_map/ppermute | solution.py:302
  20.9 8.7 %collective-permute-start.4 = (f32[64,512]{1,0:T(8,128)S(1)}, f32[64,512]{1,0:T(8,128)S(1)}, u32[]{:S(2)}, u32[]{:S(2)}) collective-permute-start(f32[64,512]{1,0:T(8,128)S(1)} %add_add_fusion), channel_id=1, source_target_pairs={{0,8},{2,10},{4,12},{6,14},{8,0},{10,2},{12,4},{14,6},{1,9},{3,11}... | collective-permute-start | bytes 393224 | tf_op jit(solution)/shard_map/ppermute | solution.py:302
  23.6 18.4 %collective-permute-start.8 = (f32[1,176,512]{2,1,0:T(8,128)S(1)}, f32[1,176,512]{2,1,0:T(8,128)S(1)}, u32[]{:S(2)}, u32[]{:S(2)}) collective-permute-start(f32[1,176,512]{2,1,0:T(8,128)S(1)} %get-tuple-element.24), channel_id=1, source_target_pairs={{2,0},{4,2},{6,4},{8,6},{10,8},{12,10},{14,12},{3,1},{5,3},{7,5},{... | collective-permute-start | bytes 1081352 | tf_op jit(solution)/shard_map/ppermute | solution.py:402
  24.9 17.1 %collective-permute-start.9 = (f32[1,80,512]{2,1,0:T(8,128)S(1)}, f32[1,80,512]{2,1,0:T(8,128)S(1)}, u32[]{:S(2)}, u32[]{:S(2)}) collective-permute-start(f32[1,80,512]{2,1,0:T(8,128)S(1)} %get-tuple-element.25), channel_id=1, source_target_pairs={{2,0},{4,2},{6,4},{8,6},{10,8},{12,10},{14,12},{3,1},{5,3},{7,5},{... | collective-permute-start | bytes 491528 | tf_op jit(solution)/shard_map/ppermute | solution.py:404
  29.7 16.6 %collective-permute-start.5 = (f32[64,512]{1,0:T(8,128)S(1)}, f32[64,512]{1,0:T(8,128)S(1)}, u32[]{:S(2)}, u32[]{:S(2)}) collective-permute-start(f32[64,512]{1,0:T(8,128)S(1)} %add_multiply_fusion.refs_1_), channel_id=1, source_target_pairs={{0,2},{2,0},{4,6},{6,4},{8,10},{10,8},{12,14},{14,12},{1,3},{3,1},... | collective-permute-start | bytes 393224 | tf_op jit(solution)/shard_map/ppermute | solution.py:302
  29.7 16.5 %collective-permute-start.6 = (f32[64,512]{1,0:T(8,128)S(1)}, f32[64,512]{1,0:T(8,128)S(1)}, u32[]{:S(2)}, u32[]{:S(2)}) collective-permute-start(f32[64,512]{1,0:T(8,128)S(1)} %add_multiply_fusion.refs_1_), channel_id=1, source_target_pairs={{0,4},{2,6},{4,0},{6,2},{8,12},{10,14},{12,8},{14,10},{1,5},{3,7},... | collective-permute-start | bytes 393224 | tf_op jit(solution)/shard_map/ppermute | solution.py:302
  31.5 14.7 %collective-permute-start.7 = (f32[64,512]{1,0:T(8,128)S(1)}, f32[64,512]{1,0:T(8,128)S(1)}, u32[]{:S(2)}, u32[]{:S(2)}) collective-permute-start(f32[64,512]{1,0:T(8,128)S(1)} %add_multiply_fusion.refs_1_), channel_id=1, source_target_pairs={{0,6},{2,4},{4,2},{6,0},{8,14},{10,12},{12,10},{14,8},{1,7},{3,5},... | collective-permute-start | bytes 393224 | tf_op jit(solution)/shard_map/ppermute | solution.py:302
  42.0 1.2 %collective-permute-start.10 = (f32[1,3,512]{2,1,0:T(4,128)S(1)}, f32[1,3,512]{2,1,0:T(4,128)S(1)}, u32[]{:S(2)}, u32[]{:S(2)}) collective-permute-start(f32[1,3,512]{2,1,0:T(4,128)S(1)} %rim.1), channel_id=1, source_target_pairs={{0,1},{1,0},{2,3},{3,2},{4,5},{5,4},{6,7},{7,6},{8,9},{9,8},{10,11... | collective-permute-start | bytes 18440 | tf_op jit(solution)/shard_map/ppermute | solution.py:429

commit v5 on v4

--- a/solution.py
+++ b/solution.py
@@ -72,8 +72,14 @@
     return pl.multiple_of((place[0] ^ k) * part_rows, SUBLANES)
 
 
-def window_kernel(k, rows_total, dates_total, place, image, above, below, sums, part, *rest):
+def window_kernel(ks, rows_total, dates_total, place, image, above, below, *rest):
     held = rest[-1]
+    for i, k in enumerate(ks):
+        sums, part = rest[2 * i : 2 * i + 2]
+        part_windows(k, rows_total, dates_total, place, image, above, below, sums, part, rest[2 * len(ks)], held)
+
+
+def part_windows(k, rows_total, dates_total, place, image, above, below, sums, part, norm, held):
     dates_n, rows_n, cols_n = image.shape
     tiles_n, part_rows = sums.shape[1], sums.shape[2]
     first = part_row(place, k, part_rows)
@@ -115,7 +121,7 @@
             count = cell_count(place[1] + first + row, j * LANES, rows_total, cols_n)
             part[pl.ds(row, SUBLANES), pl.ds(j * LANES, LANES)] = ratio[j] * count
             if k == 0:
-                rest[0][pl.ds(row, SUBLANES), pl.ds(j * LANES, LANES)] = 1.0 / (count * dates_total)
+                norm[pl.ds(row, SUBLANES), pl.ds(j * LANES, LANES)] = 1.0 / (count * dates_total)
 
 
 def fill_above(place, held, above):
@@ -137,20 +143,19 @@
 OUTER = pl.BlockSpec(memory_space=pltpu.HBM)
 
 
-def window_call(image, above, below, k, parts_n, rows_total, dates_total):
+def window_call(image, above, below, ks, parts_n, rows_total, dates_total):
     dates_n, rows_n, cols_n = image.shape
     tiles_n = cols_n // LANES
     part_rows = rows_n // parts_n
-    outs = 2 if k == 0 else 1
     f32 = jnp.float32
-    return pl.pallas_call(
-        located(functools.partial(window_kernel, k, rows_total, float(dates_total)), parts_n, rows_n),
-        out_shape=[
-            jax.ShapeDtypeStruct((dates_n, tiles_n, part_rows, LANES), f32),
-        ]
-        + [jax.ShapeDtypeStruct((part_rows, cols_n), f32)] * outs,
+    sums = jax.ShapeDtypeStruct((dates_n, tiles_n, part_rows, LANES), f32)
+    part = jax.ShapeDtypeStruct((part_rows, cols_n), f32)
+    out_shape = [sums, part] * len(ks) + [part] * (0 in ks)
+    return pl.pallas_call(
+        located(functools.partial(window_kernel, ks, rows_total, float(dates_total)), parts_n, rows_n),
+        out_shape=out_shape,
         in_specs=[WHOLE, WHOLE, WHOLE],
-        out_specs=[WHOLE] * (1 + outs),
+        out_specs=[WHOLE] * len(out_shape),
         scratch_shapes=[pltpu.VMEM((dates_n, tiles_n, part_rows + 2 * SUBLANES, LANES), f32)],
         compiler_params=pltpu.CompilerParams(vmem_limit_bytes=12 * MIB),
         cost_estimate=pl.CostEstimate(flops=500 * image.size, bytes_accessed=8 * image.size, transcendentals=0),
@@ -214,6 +219,7 @@
     fill_above(place, held, above)
     fill_below(place, held, below)
     keep = place[4] == 0
+    copies = []
     for k in range(parts_n):
         first = part_row(place, k, part_rows)
 
@@ -230,9 +236,12 @@
                     ahead = jnp.where(keep, total[j], own)
                     made[pl.ds(row, SUBLANES), pl.ds(j * LANES, LANES)] = jnp.log(ahead) - jnp.log(own)
 
-    copy = pltpu.make_async_copy(made, change.at[dates_n - 1], sem)
-    copy.start()
-    copy.wait()
+        rows = pl.ds(first, part_rows)
+        copy = pltpu.make_async_copy(made.at[rows, :], change.at[dates_n - 1, rows, :], sem.at[k])
+        copy.start()
+        copies.append(copy)
+    for copy in copies:
+        copy.wait()
 
 
 def last_call(sums, pieces, above, below, change):
@@ -249,7 +258,7 @@
         scratch_shapes=[
             pltpu.VMEM((1, tiles_n, rows_n + 2 * SUBLANES, LANES), jnp.float32),
             pltpu.VMEM((rows_n, cols_n), jnp.float32),
-            pltpu.SemaphoreType.DMA,
+            pltpu.SemaphoreType.DMA((parts_n,)),
         ],
         input_output_aliases={inputs: 0},
         compiler_params=pltpu.CompilerParams(vmem_limit_bytes=12 * MIB),
@@ -371,7 +380,7 @@
 
 
 def early_rows(rows_n):
-    cut = rows_n * 11 // 16 // SUBLANES * SUBLANES
+    cut = rows_n * 10 // 16 // SUBLANES * SUBLANES
     return cut if cut >= SUBLANES else rows_n
 
 
@@ -402,13 +411,14 @@
     after = [lax.ppermute(pieces[0], "date", route)]
     if len(pieces) > 1:
         after.append(lax.ppermute(pieces[1], "date", route))
-    sums, parts = [], []
-    for k in range(parts_n):
-        made = window_call(image, above, below, k, parts_n, rows_total, dates_total)
-        sums.append(made[0])
-        parts.append(made[1])
-        if k == 0:
-            norm = made[2]
+    others = tuple(range(1, parts_n))
+    sums, parts = [None] * parts_n, [None] * parts_n
+    for ks in (others, (0,)):
+        if ks:
+            made = window_call(image, above, below, ks, parts_n, rows_total, dates_total)
+            for i, k in enumerate(ks):
+                sums[k], parts[k] = made[2 * i : 2 * i + 2]
+    norm = made[-1]
 
     if parts_n == 1:
         total = lax.psum(parts[0], "date")

time: 48.3 us -> 49.2 us (1.019)
  waiting for transfers between devices: 14.7 us -> 15.7 us
    ppermute x7, waiting for transfers between devices: 7.01 us -> 7.75 us  [crossed(): lax.ppermute(block, axis, [(i, i ^ bits) for i in range(lax.axis_size(axi...]
    pallas_call x4 -> x2, Pallas kernels: 9.27 us -> 9.24 us  [window_call(): pl.pallas_call(located(functools.partial(window_kernel, ks, rows_total, f...]
  transfers between devices with their start and end apart: 11 -> 11, of which waited for: 5 -> 6; matrix products, arithmetic and copies ran while one was open for 0% -> 0% of each run, Pallas kernels for 27% -> 17%
where the time goes in v5:
time: 49.2 us; the launch traced here: 49 us
  Pallas kernels  18.4 us (37%)
  waiting for transfers between devices  15.7 us (32%)
  starting transfers between devices  14.1 us (29%)
  between operations  0.76 us (2%)
    ppermute x7, starting transfers between devices, crossed(): lax.ppermute(block, axis, [(i, i ^ bits) for i in range(lax.axis_size(axi...  10.8 us
    pallas_call x2, Pallas kernels, window_call(): pl.pallas_call(located(functools.partial(window_kernel, ks, rows_total, f...  9.24 us
    ppermute x7, waiting for transfers between devices, crossed(): lax.ppermute(block, axis, [(i, i ^ bits) for i in range(lax.axis_size(axi...  7.75 us
    ppermute x1, waiting for transfers between devices, on_device(): after.append(lax.ppermute(pieces[1], 'date', route))  6.92 us
    pallas_call x2, Pallas kernels, scale_call(): pl.pallas_call(located(functools.partial(scale_kernel, ks), rows_n // par...  2.92 us
    pallas_call x1, Pallas kernels, last_call(): pl.pallas_call(located(functools.partial(last_kernel, parts_n, unroll), p...  2.9 us
    pallas_call x1, Pallas kernels, change_call(): pl.pallas_call(located(functools.partial(change_kernel, parts_n), parts_n...  2.07 us
    ppermute x1, starting transfers between devices, on_device(): after.append(lax.ppermute(pieces[1], 'date', route))  1.29 us
  transfers between devices with their start and end apart: 11, of which 6 were waited for; matrix products, arithmetic and copies ran while one was open for 0% of the time, Pallas kernels for 17%

profile of v5, /device:TPU:0, one launch (start us, length us, event | category | flops | bytes accessed | tf_op | source)
XLA Modules:
  0.0 49.0 jit_solution(8922274621425129111)
XLA Ops:
  0.6 0.0 copy-start
  0.6 1.3 %prepare.1 = (f32[8,3,512]{2,1,0:T(4,128)S(1)}, f32[1,160,512]{2,1,0:T(8,128)S(1)}, f32[1,96,512]{2,1,0:T(8,128)S(1)}) custom-call(f32[8,256,512]{2,1,0:T(8,128)} %refs_0_.5), custom_call_target="tpu_custom_call" | custom-call | tf_op jit(solution)/shard_map/prepare/pallas_call | solution.py:367
  1.9 0.6 %collective-permute-start = (f32[8,3,512]{2,1,0:T(4,128)S(1)}, f32[8,3,512]{2,1,0:T(4,128)S(1)}, u32[]{:S(2)}, u32[]{:S(2)}) collective-permute-start(f32[8,3,512]{2,1,0:T(4,128)S(1)} %get-tuple-element.14), channel_id=1, source_target_pairs={{0,1},{1,0},{2,3},{3,2},{4,5},{5,4},{6,7},{7,6},{8,9},{9,8},{10,11... | collective-permute-start | bytes 147464 | tf_op jit(solution)/shard_map/ppermute | solution.py:407
  2.5 0.9 %collective-permute-done.refs_1_.refs_2_ = f32[8,3,512]{2,1,0:T(4,128)S(1)} collective-permute-done((f32[8,3,512]{2,1,0:T(4,128)S(1)}, f32[8,3,512]{2,1,0:T(4,128)S(1)}, u32[]{:S(2)}, u32[]{:S(2)}) %collective-permute-start) | collective-permute-done | bytes 49184 | tf_op jit(solution)/shard_map/ppermute | solution.py:407
  3.4 0.0 copy-done
  3.4 6.9 %shard_map.30 = (f32[8,4,64,128]{3,2,1,0:T(8,128)S(1)}, f32[64,512]{1,0:T(8,128)S(1)}, f32[8,4,64,128]{3,2,1,0:T(8,128)S(1)}, f32[64,512]{1,0:T(8,128)S(1)}, f32...) custom-call(f32[8,256,512]{2,1,0:T(8,128)S(1)} %copy-done, f32[8,3,512]{2,1,0:T(4,128)S(1)} %collective-permute-done.refs_1_.refs_2_, ...), custom_call_target="tpu_custom_call" | custom-call | flops 524288000 | bytes 8388608 | tf_op jit(solution)/shard_map/pallas_call | solution.py:154
  10.3 2.9 %collective-permute-start.1 = (f32[64,512]{1,0:T(8,128)S(1)}, f32[64,512]{1,0:T(8,128)S(1)}, u32[]{:S(2)}, u32[]{:S(2)}) collective-permute-start(f32[64,512]{1,0:T(8,128)S(1)} %get-tuple-element.19), channel_id=1, source_target_pairs={{0,2},{2,0},{4,6},{6,4},{8,10},{10,8},{12,14},{14,12},{1,3},{3,1},... | collective-permute-start | bytes 393224 | tf_op jit(solution)/shard_map/ppermute | solution.py:311
  13.2 1.6 %collective-permute-start.2 = (f32[64,512]{1,0:T(8,128)S(1)}, f32[64,512]{1,0:T(8,128)S(1)}, u32[]{:S(2)}, u32[]{:S(2)}) collective-permute-start(f32[64,512]{1,0:T(8,128)S(1)} %get-tuple-element.20), channel_id=1, source_target_pairs={{0,4},{2,6},{4,0},{6,2},{8,12},{10,14},{12,8},{14,10},{1,5},{3,7},... | collective-permute-start | bytes 393224 | tf_op jit(solution)/shard_map/ppermute | solution.py:311
  14.8 0.0 collective-permute-start.3
  14.8 2.3 %shard_map.31 = (f32[8,4,64,128]{3,2,1,0:T(8,128)S(1)}, f32[64,512]{1,0:T(8,128)S(1)}, f32[64,512]{1,0:T(8,128)S(1)}) custom-call(f32[8,256,512]{2,1,0:T(8,128)S(1)} %copy-done, f32[8,3,512]{2,1,0:T(4,128)S(1)} %collective-permute-done.refs_1_.refs_2_, f32[8,3,512]{2,1,0:T(4,128)S(1)} %collective-permute-done.refs_1_.refs_2_), custom_call_target="tpu_custom_call" | custom-call | flops 524288000 | bytes 8388608 | tf_op jit(solution)/shard_map/pallas_call | solution.py:154
  17.1 0.0 collective-permute-done.1
  17.1 2.5 %collective-permute-done.2 = f32[64,512]{1,0:T(8,128)S(1)} collective-permute-done((f32[64,512]{1,0:T(8,128)S(1)}, f32[64,512]{1,0:T(8,128)S(1)}, u32[]{:S(2)}, u32[]{:S(2)}) %collective-permute-start.2) | collective-permute-done | bytes 131104 | tf_op jit(solution)/shard_map/ppermute | solution.py:311
  19.6 1.5 %collective-permute-done.3 = f32[64,512]{1,0:T(8,128)S(1)} collective-permute-done((f32[64,512]{1,0:T(8,128)S(1)}, f32[64,512]{1,0:T(8,128)S(1)}, u32[]{:S(2)}, u32[]{:S(2)}) %collective-permute-start.3) | collective-permute-done | bytes 131104 | tf_op jit(solution)/shard_map/ppermute | solution.py:311
  21.2 2.8 %collective-permute-start.4 = (f32[64,512]{1,0:T(8,128)S(1)}, f32[64,512]{1,0:T(8,128)S(1)}, u32[]{:S(2)}, u32[]{:S(2)}) collective-permute-start(f32[64,512]{1,0:T(8,128)S(1)} %add_add_fusion), channel_id=1, source_target_pairs={{0,8},{2,10},{4,12},{6,14},{8,0},{10,2},{12,4},{14,6},{1,9},{3,11}... | collective-permute-start | bytes 393224 | tf_op jit(solution)/shard_map/ppermute | solution.py:311
  24.0 1.3 %collective-permute-start.8 = (f32[1,160,512]{2,1,0:T(8,128)S(1)}, f32[1,160,512]{2,1,0:T(8,128)S(1)}, u32[]{:S(2)}, u32[]{:S(2)}) collective-permute-start(f32[1,160,512]{2,1,0:T(8,128)S(1)} %get-tuple-element.24), channel_id=1, source_target_pairs={{2,0},{4,2},{6,4},{8,6},{10,8},{12,10},{14,12},{3,1},{5,3},{7,5},{... | collective-permute-start | bytes 983048 | tf_op jit(solution)/shard_map/ppermute | solution.py:411
  25.2 1.3 %collective-permute-start.9 = (f32[1,96,512]{2,1,0:T(8,128)S(1)}, f32[1,96,512]{2,1,0:T(8,128)S(1)}, u32[]{:S(2)}, u32[]{:S(2)}) collective-permute-start(f32[1,96,512]{2,1,0:T(8,128)S(1)} %get-tuple-element.25), channel_id=1, source_target_pairs={{2,0},{4,2},{6,4},{8,6},{10,8},{12,10},{14,12},{3,1},{5,3},{7,5},{... | collective-permute-start | bytes 589832 | tf_op jit(solution)/shard_map/ppermute | solution.py:413
  26.5 3.8 %collective-permute-done.4 = f32[64,512]{1,0:T(8,128)S(1)} collective-permute-done((f32[64,512]{1,0:T(8,128)S(1)}, f32[64,512]{1,0:T(8,128)S(1)}, u32[]{:S(2)}, u32[]{:S(2)}) %collective-permute-start.4) | collective-permute-done | bytes 131104 | tf_op jit(solution)/shard_map/ppermute | solution.py:311
  30.4 0.8 %collective-permute-start.5 = (f32[64,512]{1,0:T(8,128)S(1)}, f32[64,512]{1,0:T(8,128)S(1)}, u32[]{:S(2)}, u32[]{:S(2)}) collective-permute-start(f32[64,512]{1,0:T(8,128)S(1)} %add_multiply_fusion.refs_1_), channel_id=1, source_target_pairs={{0,2},{2,0},{4,6},{6,4},{8,10},{10,8},{12,14},{14,12},{1,3},{3,1},... | collective-permute-start | bytes 393224 | tf_op jit(solution)/shard_map/ppermute | solution.py:311
  31.1 1.8 %collective-permute-start.6 = (f32[64,512]{1,0:T(8,128)S(1)}, f32[64,512]{1,0:T(8,128)S(1)}, u32[]{:S(2)}, u32[]{:S(2)}) collective-permute-start(f32[64,512]{1,0:T(8,128)S(1)} %add_multiply_fusion.refs_1_), channel_id=1, source_target_pairs={{0,4},{2,6},{4,0},{6,2},{8,12},{10,14},{12,8},{14,10},{1,5},{3,7},... | collective-permute-start | bytes 393224 | tf_op jit(solution)/shard_map/ppermute | solution.py:311
  32.9 1.0 %collective-permute-start.7 = (f32[64,512]{1,0:T(8,128)S(1)}, f32[64,512]{1,0:T(8,128)S(1)}, u32[]{:S(2)}, u32[]{:S(2)}) collective-permute-start(f32[64,512]{1,0:T(8,128)S(1)} %add_multiply_fusion.refs_1_), channel_id=1, source_target_pairs={{0,6},{2,4},{4,2},{6,0},{8,14},{10,12},{12,10},{14,8},{1,7},{3,5},... | collective-permute-start | bytes 393224 | tf_op jit(solution)/shard_map/ppermute | solution.py:311
  33.9 2.1 %change.1.refs_8_ = f32[8,256,512]{2,1,0:T(8,128)} custom-call(f32[8,4,64,128]{3,2,1,0:T(8,128)S(1)} %get-tuple-element.23.refs_0_, f32[8,4,64,128]{3,2,1,0:T(8,128)S(1)} %get-tuple-element.15.refs_0_.refs_1_, f32[8,4,64,128]{3,2,1,0:T(8,128)S(1)} %get-tuple-element.16.refs_1_.refs_2_, f32[8,4,64,128]{3,2,1,0:T(8,128)S(1)} %get-tuple-element.17.refs_2_.refs_3_), custom_call_target="tpu_custom_call" | custom-call | flops 2097152000 | bytes 8388608 | tf_op jit(solution)/shard_map/change/pallas_call | solution.py:195
  36.0 6.9 %collective-permute-done.9.refs_1_.refs_5_ = f32[1,96,512]{2,1,0:T(8,128)S(1)} collective-permute-done((f32[1,96,512]{2,1,0:T(8,128)S(1)}, f32[1,96,512]{2,1,0:T(8,128)S(1)}, u32[]{:S(2)}, u32[]{:S(2)}) %collective-permute-start.9) | collective-permute-done | bytes 196640 | tf_op jit(solution)/shard_map/ppermute | solution.py:413
  42.9 0.0 collective-permute-done.8.refs_0_.refs_4_
  42.9 0.1 collective-permute-start.10
  43.0 1.0 %shard_map.32.refs_6_ = f32[8,256,512]{2,1,0:T(8,128)} custom-call(f32[8,4,64,128]{3,2,1,0:T(8,128)S(1)} %get-tuple-element.23.refs_0_, f32[64,512]{1,0:T(8,128)S(1)} %add_multiply_fusion.refs_1_), custom_call_target="tpu_custom_call" | custom-call | flops 262144000 | bytes 2097152 | tf_op jit(solution)/shard_map/pallas_call | solution.py:295
  44.0 0.1 collective-permute-done.10.refs_6_.refs_7_
  44.2 2.9 %last.1 = f32[8,256,512]{2,1,0:T(8,128)} custom-call(f32[8,4,64,128]{3,2,1,0:T(8,128)S(1)} %get-tuple-element.23.refs_0_, f32[8,4,64,128]{3,2,1,0:T(8,128)S(1)} %get-tuple-element.15.refs_0_.refs_1_, f32[8,4,64,128]{3,2,1,0:T(8,128)S(1)} %get-tuple-element.16.refs_1_.refs_2_, ...), custom_call_target="tpu_custom_call", output_to_operand_aliasing={{}: (8, {})} | custom-call | flops 262144000 | bytes 1572864 | tf_op jit(solution)/shard_map/last/pallas_call | solution.py:253
  47.1 0.0 collective-permute-done.5.refs_3_
  47.1 0.0 collective-permute-done.6.refs_4_
  47.1 0.0 collective-permute-done.7.refs_5_
  47.1 1.9 %shard_map.33 = f32[8,256,512]{2,1,0:T(8,128)} custom-call(f32[8,4,64,128]{3,2,1,0:T(8,128)S(1)} %get-tuple-element.15.refs_0_.refs_1_, f32[8,4,64,128]{3,2,1,0:T(8,128)S(1)} %get-tuple-element.16.refs_1_.refs_2_, f32[8,4,64,128]{3,2,1,0:T(8,128)S(1)} %get-tuple-element.17.refs_2_.refs_3_, ...), custom_call_target="tpu_custom_call", output_to_operand_aliasing={{}: (6, {})} | custom-call | flops 786432000 | bytes 6291456 | tf_op jit(solution)/shard_map/pallas_call | solution.py:295
  (3 shorter events, 0.1 us)
Async XLA Ops:
  0.6 2.8 %copy-start = (f32[8,256,512]{2,1,0:T(8,128)S(1)}, f32[8,256,512]{2,1,0:T(8,128)}, u32[]{:S(2)}) copy-start(f32[8,256,512]{2,1,0:T(8,128)} %refs_0_.5) | copy-start | bytes 12582916
  1.9 1.5 %collective-permute-start = (f32[8,3,512]{2,1,0:T(4,128)S(1)}, f32[8,3,512]{2,1,0:T(4,128)S(1)}, u32[]{:S(2)}, u32[]{:S(2)}) collective-permute-start(f32[8,3,512]{2,1,0:T(4,128)S(1)} %get-tuple-element.14), channel_id=1, source_target_pairs={{0,1},{1,0},{2,3},{3,2},{4,5},{5,4},{6,7},{7,6},{8,9},{9,8},{10,11... | collective-permute-start | bytes 147464 | tf_op jit(solution)/shard_map/ppermute | solution.py:407
  10.3 6.8 %collective-permute-start.1 = (f32[64,512]{1,0:T(8,128)S(1)}, f32[64,512]{1,0:T(8,128)S(1)}, u32[]{:S(2)}, u32[]{:S(2)}) collective-permute-start(f32[64,512]{1,0:T(8,128)S(1)} %get-tuple-element.19), channel_id=1, source_target_pairs={{0,2},{2,0},{4,6},{6,4},{8,10},{10,8},{12,14},{14,12},{1,3},{3,1},... | collective-permute-start | bytes 393224 | tf_op jit(solution)/shard_map/ppermute | solution.py:311
  13.2 6.4 %collective-permute-start.2 = (f32[64,512]{1,0:T(8,128)S(1)}, f32[64,512]{1,0:T(8,128)S(1)}, u32[]{:S(2)}, u32[]{:S(2)}) collective-permute-start(f32[64,512]{1,0:T(8,128)S(1)} %get-tuple-element.20), channel_id=1, source_target_pairs={{0,4},{2,6},{4,0},{6,2},{8,12},{10,14},{12,8},{14,10},{1,5},{3,7},... | collective-permute-start | bytes 393224 | tf_op jit(solution)/shard_map/ppermute | solution.py:311
  14.8 6.3 %collective-permute-start.3 = (f32[64,512]{1,0:T(8,128)S(1)}, f32[64,512]{1,0:T(8,128)S(1)}, u32[]{:S(2)}, u32[]{:S(2)}) collective-permute-start(f32[64,512]{1,0:T(8,128)S(1)} %get-tuple-element.21), channel_id=1, source_target_pairs={{0,6},{2,4},{4,2},{6,0},{8,14},{10,12},{12,10},{14,8},{1,7},{3,5},... | collective-permute-start | bytes 393224 | tf_op jit(solution)/shard_map/ppermute | solution.py:311
  21.2 9.2 %collective-permute-start.4 = (f32[64,512]{1,0:T(8,128)S(1)}, f32[64,512]{1,0:T(8,128)S(1)}, u32[]{:S(2)}, u32[]{:S(2)}) collective-permute-start(f32[64,512]{1,0:T(8,128)S(1)} %add_add_fusion), channel_id=1, source_target_pairs={{0,8},{2,10},{4,12},{6,14},{8,0},{10,2},{12,4},{14,6},{1,9},{3,11}... | collective-permute-start | bytes 393224 | tf_op jit(solution)/shard_map/ppermute | solution.py:311
  24.0 18.9 %collective-permute-start.8 = (f32[1,160,512]{2,1,0:T(8,128)S(1)}, f32[1,160,512]{2,1,0:T(8,128)S(1)}, u32[]{:S(2)}, u32[]{:S(2)}) collective-permute-start(f32[1,160,512]{2,1,0:T(8,128)S(1)} %get-tuple-element.24), channel_id=1, source_target_pairs={{2,0},{4,2},{6,4},{8,6},{10,8},{12,10},{14,12},{3,1},{5,3},{7,5},{... | collective-permute-start | bytes 983048 | tf_op jit(solution)/shard_map/ppermute | solution.py:411
  25.2 17.7 %collective-permute-start.9 = (f32[1,96,512]{2,1,0:T(8,128)S(1)}, f32[1,96,512]{2,1,0:T(8,128)S(1)}, u32[]{:S(2)}, u32[]{:S(2)}) collective-permute-start(f32[1,96,512]{2,1,0:T(8,128)S(1)} %get-tuple-element.25), channel_id=1, source_target_pairs={{2,0},{4,2},{6,4},{8,6},{10,8},{12,10},{14,12},{3,1},{5,3},{7,5},{... | collective-permute-start | bytes 589832 | tf_op jit(solution)/shard_map/ppermute | solution.py:413
  30.4 16.7 %collective-permute-start.5 = (f32[64,512]{1,0:T(8,128)S(1)}, f32[64,512]{1,0:T(8,128)S(1)}, u32[]{:S(2)}, u32[]{:S(2)}) collective-permute-start(f32[64,512]{1,0:T(8,128)S(1)} %add_multiply_fusion.refs_1_), channel_id=1, source_target_pairs={{0,2},{2,0},{4,6},{6,4},{8,10},{10,8},{12,14},{14,12},{1,3},{3,1},... | collective-permute-start | bytes 393224 | tf_op jit(solution)/shard_map/ppermute | solution.py:311
  31.1 15.9 %collective-permute-start.6 = (f32[64,512]{1,0:T(8,128)S(1)}, f32[64,512]{1,0:T(8,128)S(1)}, u32[]{:S(2)}, u32[]{:S(2)}) collective-permute-start(f32[64,512]{1,0:T(8,128)S(1)} %add_multiply_fusion.refs_1_), channel_id=1, source_target_pairs={{0,4},{2,6},{4,0},{6,2},{8,12},{10,14},{12,8},{14,10},{1,5},{3,7},... | collective-permute-start | bytes 393224 | tf_op jit(solution)/shard_map/ppermute | solution.py:311
  32.9 14.2 %collective-permute-start.7 = (f32[64,512]{1,0:T(8,128)S(1)}, f32[64,512]{1,0:T(8,128)S(1)}, u32[]{:S(2)}, u32[]{:S(2)}) collective-permute-start(f32[64,512]{1,0:T(8,128)S(1)} %add_multiply_fusion.refs_1_), channel_id=1, source_target_pairs={{0,6},{2,4},{4,2},{6,0},{8,14},{10,12},{12,10},{14,8},{1,7},{3,5},... | collective-permute-start | bytes 393224 | tf_op jit(solution)/shard_map/ppermute | solution.py:311
  42.9 1.2 %collective-permute-start.10 = (f32[1,3,512]{2,1,0:T(4,128)S(1)}, f32[1,3,512]{2,1,0:T(4,128)S(1)}, u32[]{:S(2)}, u32[]{:S(2)}) collective-permute-start(f32[1,3,512]{2,1,0:T(4,128)S(1)} %rim.1), channel_id=1, source_target_pairs={{0,1},{1,0},{2,3},{3,2},{4,5},{5,4},{6,7},{7,6},{8,9},{9,8},{10,11... | collective-permute-start | bytes 18440 | tf_op jit(solution)/shard_map/ppermute | solution.py:439
